TPU v7x, 256 devices: a whole 4x4x8 slice. The times are simulated.
256 devices in a mesh: gx: 8 (over y, core), gy: 32 (over x, z).
Axes of the slice: x: 4, y: 4, z: 8, core: 2. Of those that a mesh axis runs over, the one named last changes fastest.
Arguments:
- previous: float32 [2, 7, 1024, 4096], P(None, None, 'gx', 'gy'), may hold values from -6 to 6
- dissipated: float32 [2, 4, 1024, 4096], P(None, None, 'gx', 'gy'), may hold values from 0.05 to 3
- material: int32 [4, 1024, 4096], P(None, 'gx', 'gy'), may hold values from 0 to 3
- coolant: int32 [3, 1024, 4096], P(None, 'gx', 'gy'), may hold values from 0 to 3
Outputs:
- temperature: float32 [2, 7, 1024, 4096], P(None, None, 'gx', 'gy')
All inputs are finite; a program needn't handle non-finite values.
Results may differ from a plain program's by a relative error of at most 0.00011.
Values sent between devices are 32-bit elements; how exact they have to be, the bound alone decides.
No kernel may reach another device: no remote copies, remote signals or barrier semaphores. Data moves between devices by JAX's collectives and lax.ppermute only.
A program may use at most 64 MiB of HBM per device.

v0:
```python
import jax
import jax.numpy as jnp
from jax import lax
from jax.sharding import Mesh
from jax.sharding import PartitionSpec as P

ITERS = 3
GX = ("gx_0", "gx_1")
GY = ("gy_0", "gy_1")


TIER_K = (1.0, 0.3, 0.12, 2.5)
CHANNEL_K = (1.0, 0.3, 0.25, 0.2)
CHANNEL_SINK = (0.0, 0.15, 0.45, 1.2)
TIER_HEAT = 0.05
CHANNEL_HEAT = 0.2
VERTICAL = 4.0


def sent_to_all(x, axis):
    copies = jnp.broadcast_to(x, (lax.axis_size(axis), *x.shape))
    return lax.all_to_all(copies, axis, split_axis=0, concat_axis=0, tiled=True)


def over_copies(x, axis):
    everything = sent_to_all(x, axis)
    return jnp.sum(everything, axis=0)


def over_axes(x, axes):
    far, near = axes
    nearer = over_copies(x, near)
    return over_copies(nearer, far)


def together(arrays, axis):
    ends = [0]
    for a in arrays:
        ends.append(ends[-1] + a.size)
    subtotal = over_axes(jnp.concatenate([a.ravel() for a in arrays]), axis)
    return tuple((subtotal[b:e].reshape(a.shape) for a, b, e in zip(arrays, ends, ends[1:])))


def extended_2(x, sides, width):
    edges = {}
    for axis, dim in sides:
        devices, length = (lax.axis_size(axis), x.shape[dim])
        up = [(i, (i + 1) % devices) for i in range(devices - 1)]
        last = lax.slice_in_dim(x, length - width, length, axis=dim)
        leading = lax.slice_in_dim(x, 0, width, axis=dim)
        edges[dim] = (
            lax.ppermute(last, axis, up),
            lax.ppermute(leading, axis, [(b, a) for a, b in up]),
        )
    done = []
    for _, dim in sides:
        low, high = edges[dim]
        around = [(width, width) if d in done else (0, 0) for d in range(x.ndim)]
        x = jnp.concatenate([jnp.pad(low, around), x, jnp.pad(high, around)], axis=dim)
        done.append(dim)
    return x


def lookup(codes, table):
    total = jnp.zeros(codes.shape, jnp.float32)
    for index, value in enumerate(table):
        total = total + jnp.where(codes == index, jnp.float32(value), jnp.float32(0.0))
    return total


def mix(tiers, channels):
    rows = []
    for layer in range(2 * tiers.shape[0] - 1):
        rows.append(tiers[layer // 2] if layer % 2 == 0 else channels[layer // 2])
    return jnp.stack(rows)


def spread_power(heat):
    tiers = heat.shape[1]
    empty = jnp.zeros_like(heat[:, 0])
    rows = []
    for layer in range(2 * tiers - 1):
        rows.append(heat[:, layer // 2] if layer % 2 == 0 else empty)
    return jnp.stack(rows, 1)


def capacity_column(layers):
    return jnp.array(
        [TIER_HEAT if layer % 2 == 0 else CHANNEL_HEAT for layer in range(layers)], jnp.float32
    )


def couplings(padded_k):
    centre = padded_k[:, 1:-1, 1:-1]
    g_north = jnp.sqrt(centre * padded_k[:, :-2, 1:-1])
    g_south = jnp.sqrt(centre * padded_k[:, 2:, 1:-1])
    g_west = jnp.sqrt(centre * padded_k[:, 1:-1, :-2])
    g_east = jnp.sqrt(centre * padded_k[:, 1:-1, 2:])
    g_vertical = VERTICAL * jnp.sqrt(centre[:-1] * centre[1:])
    return (g_north, g_south, g_west, g_east, g_vertical)


def operate(padded_v, padded_k, sink, capacity):
    g_north, g_south, g_west, g_east, g_vertical = couplings(padded_k)
    centre = padded_v[:, :, 1:-1, 1:-1]
    lateral = g_north * (centre - padded_v[:, :, :-2, 1:-1]) + g_south * (
        centre - padded_v[:, :, 2:, 1:-1]
    )
    lateral = (
        lateral
        + g_west * (centre - padded_v[:, :, 1:-1, :-2])
        + g_east * (centre - padded_v[:, :, 1:-1, 2:])
    )
    flux = g_vertical * (centre[:, :-1] - centre[:, 1:])
    zero_row = jnp.zeros_like(centre[:, :1])
    vertical = jnp.concatenate([flux, zero_row], 1) - jnp.concatenate([zero_row, flux], 1)
    return (capacity + sink) * centre + lateral + vertical


def diagonal_terms(padded_k, sink, capacity):
    g_north, g_south, g_west, g_east, g_vertical = couplings(padded_k)
    zero_row = jnp.zeros_like(g_vertical[:1])
    vertical = jnp.concatenate([g_vertical, zero_row], 0) + jnp.concatenate(
        [zero_row, g_vertical], 0
    )
    return capacity + sink + g_north + g_south + g_west + g_east + vertical


def core_sum(first, second):
    return jnp.sum(first * second, axis=(1, 2, 3))


def both_sums(residual, scaled, image):
    return together(
        (core_sum(residual, scaled), core_sum(scaled, image)), (("gx_0", "gx_1"), ("gy_0", "gy_1"))
    )


def per_device(previous, dissipated, material, coolant):
    tiers = material.shape[0]
    layers = 2 * tiers - 1
    capacity = capacity_column(layers)[:, None, None]
    tier_k = lookup(material, TIER_K)
    kappa = mix(tier_k, lookup(coolant, CHANNEL_K))
    channel_sink = lookup(coolant, CHANNEL_SINK)
    conductivity = extended_2(kappa, ((GX, 1), (GY, 2)), 1)
    coolant_sink = mix(jnp.zeros_like(tier_k), channel_sink)
    margin_start = 0

    def apply_operator(field, margin):
        extended = extended_2(field, ((GX, 2), (GY, 3)), 1)
        result = operate(extended, conductivity, coolant_sink, capacity)
        return (result, margin)

    diagonal = diagonal_terms(conductivity, coolant_sink, capacity)
    source = capacity * previous + spread_power(dissipated)
    image, margin = apply_operator(previous, margin_start)
    residual = source - image
    solution = previous
    scaled = residual / diagonal
    image, inner_margin = apply_operator(scaled, margin)
    energy, curvature_now = both_sums(residual, scaled, image)
    step_size = energy / curvature_now
    direction = scaled
    along = image
    margin = inner_margin
    for iteration in range(ITERS):
        solution = solution + step_size[:, None, None, None] * direction
        residual = residual - step_size[:, None, None, None] * along
        if iteration + 1 < ITERS:
            scaled = residual / diagonal
            image, inner_margin = apply_operator(scaled, margin)
            energy_next, curvature_now = both_sums(residual, scaled, image)
            growth = energy_next / energy
            step_size = energy_next / (curvature_now - growth * energy_next / step_size)
            factor = growth[:, None, None, None]
            direction = scaled + factor * direction
            along = image + factor * along
            margin = inner_margin
            energy = energy_next
    return solution


def solution(mesh):
    finer = Mesh(mesh.devices.reshape(4, 2, 4, 8), ("gx_0", "gx_1", "gy_0", "gy_1"))
    placed = (P(None, None, GX, GY), P(None, None, GX, GY), P(None, GX, GY), P(None, GX, GY))
    return jax.shard_map(
        per_device, mesh=finer, in_specs=placed, out_specs=P(None, None, GX, GY), check_vma=False
    )
```

profile of v0, /device:TPU:1, one launch (start us, length us, event | category | flops | bytes accessed | tf_op | source)
XLA Modules:
  0.0 229.0 jit_solution(17528732379370630224)
XLA Ops:
  2.8 5.1 %collective-permute-start.2 = (f32[7,1,128]{2,1,0:T(1,128)}, f32[7,1,128]{2,1,0:T(1,128)}, u32[]{:S(2)}, u32[]{:S(2)}) collective-permute-start(f32[7,1,128]{2,1,0:T(1,128)} %get-tuple-element.48), channel_id=1, source_target_pairs={{32,0},{64,32},{96,64},{128,96},{160,128},{192,160},{224,192},{33,... | collective-permute-start | bytes 10760 | tf_op jit(solution)/shard_map/ppermute | solution.py:53
  7.9 1.9 collective-permute-start
  12.2 4.8 %collective-permute-start.4 = (f32[7,128,1]{2,1,0:T(8,128)}, f32[7,128,1]{2,1,0:T(8,128)}, u32[]{:S(2)}, u32[]{:S(2)}) collective-permute-start(f32[7,128,1]{2,1,0:T(8,128)} %get-tuple-element.47), channel_id=1, source_target_pairs={{0,1},{1,2},{2,3},{3,4},{4,5},{5,6},{6,7},{7,8},{8,9},{9,10},{10,1... | collective-permute-start | bytes 10760 | tf_op jit(solution)/shard_map/ppermute | solution.py:52
  18.2 3.5 %collective-permute-start.3 = (f32[2,7,1,128]{3,1,2,0:T(8,128)}, f32[2,7,1,128]{3,1,2,0:T(8,128)S(1)}, u32[]{:S(2)}, u32[]{:S(2)}) collective-permute-start(f32[2,7,1,128]{3,1,2,0:T(8,128)} %get-tuple-element.37), channel_id=1, source_target_pairs={{32,0},{64,32},{96,64},{128,96},{160,128},{192,160},{224,192},{33,... | collective-permute-start | bytes 21512 | tf_op jit(solution)/shard_map/ppermute | solution.py:53
  30.4 2.1 copy.210
  32.9 3.6 %stack.15 = f32[2,7,128,128]{3,1,2,0:T(8,128)} concatenate(f32[2,1,128,128]{3,1,2,0:T(1,128)} %bitcast.6, f32[2,1,128,128]{3,1,2,0:T(1,128)S(1)} %broadcast.110, f32[2,1,128,128]{3,1,2,0:T(1,128)} %bitcast.5, f32[2,1,128,128]{3,1,2,0:T(1,128)S(1)} %broadcast.110, f32[2,1,128,128]{3,1,2,0:T(1,128)} %bitcast.7, f32[2,1,128,128]{3,1,2,0:T(1,128)S(1)} %broadcast.110, ...), dimensions={1} | concatenate | bytes 1835008 | tf_op jit(solution)/shard_map/stack | solution.py:84
  36.5 2.0 collective-permute-start.1
  39.8 4.0 %collective-permute-start.5 = (f32[2,7,128,1]{2,1,3,0:T(8,128)}, f32[2,7,128,1]{2,1,3,0:T(8,128)S(1)}, u32[]{:S(2)}, u32[]{:S(2)}) collective-permute-start(f32[2,7,128,1]{2,1,3,0:T(8,128)} %copy.210), channel_id=1, source_target_pairs={{0,1},{1,2},{2,3},{3,4},{4,5},{5,6},{6,7},{7,8},{8,9},{9,10},{10,1... | collective-permute-start | bytes 21512 | tf_op jit(solution)/shard_map/ppermute | solution.py:52
  43.9 2.1 add_add_fusion
  52.3 1.5 constant_dynamic-update-slice_fusion.10
  53.9 1.4 copy.218
  57.2 5.7 %broadcast_divide_fusion.2 = (f32[2,7,128,128]{3,1,2,0:T(8,128)S(1)}, f32[2,7,128,128]{3,1,2,0:T(8,128)S(1)}) fusion(f32[7,128,128]{2,0,1:T(8,128)S(1)} %copy.183, f32[2,6,128,128]{3,1,2,0:T(8,128)} %fusion.49, f32[2,7,128,128]{3,1,2,0:T(8,128)} %copy-done.3, f32[2,7,128,1]{3,1,2,0:T(8,128)} %copy.219, ...), kind=kLoop, calls=%fused_computation.111 | loop fusion | flops 6651904 | bytes 8169500 | tf_op jit(solution)/shard_map/div | solution.py:160
  62.9 1.7 fusion.86
  64.6 2.5 %collective-permute-start.8 = (f32[2,7,1,128]{3,1,2,0:T(8,128)S(1)}, f32[2,7,1,128]{3,1,2,0:T(8,128)S(1)}, u32[]{:S(2)}, u32[]{:S(2)}) collective-permute-start(f32[2,7,1,128]{3,1,2,0:T(8,128)S(1)} %get-tuple-element.35), channel_id=1, source_target_pairs={{0,32},{32,64},{64,96},{96,128},{128,160},{160,192},{192,224},{1,3... | collective-permute-start | bytes 21512 | tf_op jit(solution)/shard_map/ppermute | solution.py:52
  67.0 1.9 collective-permute-start.9
  69.0 1.6 copy.184
  70.5 1.6 copy.186
  73.4 4.0 %collective-permute-start.10 = (f32[2,7,128,1]{2,1,3,0:T(8,128)S(1)}, f32[2,7,128,1]{2,1,3,0:T(8,128)S(1)}, u32[]{:S(2)}, u32[]{:S(2)}) collective-permute-start(f32[2,7,128,1]{2,1,3,0:T(8,128)S(1)} %copy.184), channel_id=1, source_target_pairs={{0,1},{1,2},{2,3},{3,4},{4,5},{5,6},{6,7},{7,8},{8,9},{9,10},{10,1... | collective-permute-start | bytes 21512 | tf_op jit(solution)/shard_map/ppermute | solution.py:52
  78.5 1.4 copy.185
  79.9 1.4 copy.187
  81.3 4.6 %multiply_reduce_fusion.4 = (f32[2]{0:T(128)S(1)}, f32[2]{0:T(128)S(1)}, f32[2,7,128,128]{3,1,2,0:T(8,128)}) fusion(f32[2,7,128,128]{3,1,2,0:T(8,128)S(1)} %get-tuple-element.19, f32[2,7,128,128]{3,1,2,0:T(8,128)S(1)} %get-tuple-element.18, f32[2,6,128,128]{3,1,2,0:T(8,128)} %fusion.33, f32[2,7,128,1]{3,1,2,0:T(8,128)} %copy.187, ...), kind=kLoop, calls=%fused_computation.107 | loop fusion | flops 7569404 | bytes 5861392 | tf_op jit(solution)/shard_map/reduce_sum | solution.py:130
  85.9 23.7 %all_to_all.36 = f32[32,1,4]{2,1,0:T(1,128)S(1)} all-to-all(f32[32,1,4]{2,1,0:T(1,128)S(1)} %broadcast_in_dim.120), channel_id=1, replica_groups=mesh['gx_0'=4,'gx_1'=2,'gy_0'=4,'gy_1'=8] {'gy_0','gy_1'}, dimensions={0} | all-to-all | bytes 1024 | tf_op jit(solution)/shard_map/all_to_all | solution.py:22
  109.7 12.1 %all_to_all.37 = f32[8,1,4]{2,1,0:T(1,128)S(1)} all-to-all(f32[8,1,4]{2,1,0:T(1,128)S(1)} %broadcast_in_dim.121), channel_id=1, replica_groups=mesh['gx_0'=4,'gx_1'=2,'gy_0'=4,'gy_1'=8] {'gx_0','gx_1'}, dimensions={0} | all-to-all | bytes 256 | tf_op jit(solution)/shard_map/all_to_all | solution.py:22
  121.9 1.6 broadcast_divide_fusion.1
  123.6 1.7 fusion.84
  125.2 2.8 %collective-permute-start.12 = (f32[2,7,1,128]{3,1,2,0:T(8,128)S(1)}, f32[2,7,1,128]{3,1,2,0:T(8,128)S(1)}, u32[]{:S(2)}, u32[]{:S(2)}) collective-permute-start(f32[2,7,1,128]{3,1,2,0:T(8,128)S(1)} %get-tuple-element.31), channel_id=1, source_target_pairs={{0,32},{32,64},{64,96},{96,128},{128,160},{160,192},{192,224},{1,3... | collective-permute-start | bytes 21512 | tf_op jit(solution)/shard_map/ppermute | solution.py:52
  128.0 1.9 collective-permute-start.13
  129.9 1.6 copy.191
  131.5 1.6 copy.193
  134.3 4.0 %collective-permute-start.14 = (f32[2,7,128,1]{2,1,3,0:T(8,128)S(1)}, f32[2,7,128,1]{2,1,3,0:T(8,128)S(1)}, u32[]{:S(2)}, u32[]{:S(2)}) collective-permute-start(f32[2,7,128,1]{2,1,3,0:T(8,128)S(1)} %copy.191), channel_id=1, source_target_pairs={{0,1},{1,2},{2,3},{3,4},{4,5},{5,6},{6,7},{7,8},{8,9},{9,10},{10,1... | collective-permute-start | bytes 21512 | tf_op jit(solution)/shard_map/ppermute | solution.py:52
  138.3 2.2 fusion.17
  141.9 1.4 copy.194
  143.2 5.1 %multiply_reduce_fusion.2 = (f32[2]{0:T(128)S(1)}, f32[2]{0:T(128)S(1)}, f32[2,7,128,128]{3,1,2,0:T(8,128)}) fusion(f32[2,7,128,128]{3,1,2,0:T(8,128)S(1)} %broadcast_divide_fusion.1, f32[2,7,128,128]{3,1,2,0:T(8,128)S(1)} %get-tuple-element.19, f32[2,7,128,128]{3,1,2,0:T(8,128)} %get-tuple-element.17, f32[2]{0:T(128)S(1)} %slice_divide_fusion.1, ...), kind=kLoop, calls=%fused_computation.104 | loop fusion | flops 8028156 | bytes 6778904 | tf_op jit(solution)/shard_map/reduce_sum | solution.py:130
  148.4 13.7 %all_to_all.38 = f32[32,1,4]{2,1,0:T(1,128)S(1)} all-to-all(f32[32,1,4]{2,1,0:T(1,128)S(1)} %broadcast_in_dim.122), channel_id=1, replica_groups=mesh['gx_0'=4,'gx_1'=2,'gy_0'=4,'gy_1'=8] {'gy_0','gy_1'}, dimensions={0} | all-to-all | bytes 1024 | tf_op jit(solution)/shard_map/all_to_all | solution.py:22
  162.2 11.2 %all_to_all.39 = f32[8,1,4]{2,1,0:T(1,128)S(1)} all-to-all(f32[8,1,4]{2,1,0:T(1,128)S(1)} %broadcast_in_dim.123), channel_id=1, replica_groups=mesh['gx_0'=4,'gx_1'=2,'gy_0'=4,'gy_1'=8] {'gx_0','gx_1'}, dimensions={0} | all-to-all | bytes 256 | tf_op jit(solution)/shard_map/all_to_all | solution.py:22
  173.5 2.3 multiply_reduce_fusion
  176.8 1.7 fusion.82
  178.4 2.8 %collective-permute-start.16 = (f32[2,7,1,128]{3,1,2,0:T(8,128)S(1)}, f32[2,7,1,128]{3,1,2,0:T(8,128)S(1)}, u32[]{:S(2)}, u32[]{:S(2)}) collective-permute-start(f32[2,7,1,128]{3,1,2,0:T(8,128)S(1)} %get-tuple-element.27), channel_id=1, source_target_pairs={{0,32},{32,64},{64,96},{96,128},{128,160},{160,192},{192,224},{1,3... | collective-permute-start | bytes 21512 | tf_op jit(solution)/shard_map/ppermute | solution.py:52
  181.2 1.9 collective-permute-start.17
  183.1 1.6 copy.197
  184.7 1.6 copy.199
  187.5 4.0 %collective-permute-start.18 = (f32[2,7,128,1]{2,1,3,0:T(8,128)S(1)}, f32[2,7,128,1]{2,1,3,0:T(8,128)S(1)}, u32[]{:S(2)}, u32[]{:S(2)}) collective-permute-start(f32[2,7,128,1]{2,1,3,0:T(8,128)S(1)} %copy.197), channel_id=1, source_target_pairs={{0,1},{1,2},{2,3},{3,4},{4,5},{5,6},{6,7},{7,8},{8,9},{9,10},{10,1... | collective-permute-start | bytes 21512 | tf_op jit(solution)/shard_map/ppermute | solution.py:52
  191.5 2.2 fusion
  193.7 1.4 copy.198
  196.4 3.9 %fusion.64 = f32[2]{0:T(128)S(1)} fusion(f32[2,7,128,128]{3,1,2,0:T(8,128)S(1)} %broadcast_divide_fusion, f32[2,6,128,128]{3,1,2,0:T(8,128)} %fusion, f32[2,7,128,1]{3,1,2,0:T(8,128)} %copy.200, f32[2,7,1,128]{3,1,2,0:T(8,128)S(1)} %collective-permute-done.17, f32[2,7,1,128]{3,1,2,0:T(8,128)S(1)} %collective-permute-done.16, f32[2,7,128,1]{3,1,2,0:T(8,128)} %copy.198, ...), kind=kLoop, calls=%fused_computation.108 | loop fusion | flops 7110654 | bytes 4026376 | tf_op jit(solution)/shard_map/reduce_sum | solution.py:130
  200.4 13.7 %all_to_all.40 = f32[32,1,4]{2,1,0:T(1,128)S(1)} all-to-all(f32[32,1,4]{2,1,0:T(1,128)S(1)} %broadcast_in_dim.124), channel_id=1, replica_groups=mesh['gx_0'=4,'gx_1'=2,'gy_0'=4,'gy_1'=8] {'gy_0','gy_1'}, dimensions={0} | all-to-all | bytes 1024 | tf_op jit(solution)/shard_map/all_to_all | solution.py:22
  214.2 11.2 %all_to_all.41 = f32[8,1,4]{2,1,0:T(1,128)S(1)} all-to-all(f32[8,1,4]{2,1,0:T(1,128)S(1)} %broadcast_in_dim.125), channel_id=1, replica_groups=mesh['gx_0'=4,'gx_1'=2,'gy_0'=4,'gy_1'=8] {'gx_0','gx_1'}, dimensions={0} | all-to-all | bytes 256 | tf_op jit(solution)/shard_map/all_to_all | solution.py:22
  225.5 2.4 %multiply_add_fusion = f32[2,7,128,128]{3,1,2,0:T(8,128)S(1)} fusion(f32[2,7,128,128]{3,1,2,0:T(8,128)S(1)} %broadcast_divide_fusion.1, f32[2,7,128,128]{3,1,2,0:T(8,128)S(1)} %get-tuple-element.18, f32[2]{0:T(128)S(1)} %get-tuple-element.10, f32[2]{0:T(128)S(1)} %get-tuple-element.9, f32[2]{0:T(128)S(1)} %get-tuple-element.15, f32[2]{0:T(128)S(1)} %get-tuple-element.13, ...), kind=kLoop, calls=%fused_computation.100 | loop fusion | flops 2523136 | bytes 5046312 | tf_op jit(solution)/shard_map/add | solution.py:168
  (113 shorter events, 35.6 us)
Async XLA Ops:
  2.2 14.8 %copy-start = (f32[2,7,128,128]{3,2,1,0:T(8,128)S(1)}, f32[2,7,128,128]{3,2,1,0:T(8,128)}, u32[]{:S(2)}) copy-start(f32[2,7,128,128]{3,2,1,0:T(8,128)} %param.5) | copy-start | bytes 2752516
  2.8 33.7 %collective-permute-start.2 = (f32[7,1,128]{2,1,0:T(1,128)}, f32[7,1,128]{2,1,0:T(1,128)}, u32[]{:S(2)}, u32[]{:S(2)}) collective-permute-start(f32[7,1,128]{2,1,0:T(1,128)} %get-tuple-element.48), channel_id=1, source_target_pairs={{32,0},{64,32},{96,64},{128,96},{160,128},{192,160},{224,192},{33,... | collective-permute-start | bytes 10760 | tf_op jit(solution)/shard_map/ppermute | solution.py:53
  7.9 30.6 %collective-permute-start = (f32[7,1,128]{2,1,0:T(1,128)}, f32[7,1,128]{2,1,0:T(1,128)}, u32[]{:S(2)}, u32[]{:S(2)}) collective-permute-start(f32[7,1,128]{2,1,0:T(1,128)} %get-tuple-element.49), channel_id=1, source_target_pairs={{0,32},{32,64},{64,96},{96,128},{128,160},{160,192},{192,224},{1,3... | collective-permute-start | bytes 10760 | tf_op jit(solution)/shard_map/ppermute | solution.py:52
  10.9 28.9 %collective-permute-start.6 = (f32[7,128,1]{2,1,0:T(8,128)}, f32[7,128,1]{2,1,0:T(8,128)}, u32[]{:S(2)}, u32[]{:S(2)}) collective-permute-start(f32[7,128,1]{2,1,0:T(8,128)} %get-tuple-element.46), channel_id=1, source_target_pairs={{1,0},{2,1},{3,2},{4,3},{5,4},{6,5},{7,6},{8,7},{9,8},{10,9},{11,1... | collective-permute-start | bytes 10760 | tf_op jit(solution)/shard_map/ppermute | solution.py:53
  12.2 31.6 %collective-permute-start.4 = (f32[7,128,1]{2,1,0:T(8,128)}, f32[7,128,1]{2,1,0:T(8,128)}, u32[]{:S(2)}, u32[]{:S(2)}) collective-permute-start(f32[7,128,1]{2,1,0:T(8,128)} %get-tuple-element.47), channel_id=1, source_target_pairs={{0,1},{1,2},{2,3},{3,4},{4,5},{5,6},{6,7},{7,8},{8,9},{9,10},{10,1... | collective-permute-start | bytes 10760 | tf_op jit(solution)/shard_map/ppermute | solution.py:52
  17.5 11.1 %copy-start.3 = (f32[2,7,128,128]{3,1,2,0:T(8,128)}, f32[2,7,128,128]{3,1,2,0:T(8,128)S(1)}, u32[]{:S(2)}) copy-start(f32[2,7,128,128]{3,1,2,0:T(8,128)S(1)} %copy.190) | copy-start | bytes 2752516
  18.2 38.4 %collective-permute-start.3 = (f32[2,7,1,128]{3,1,2,0:T(8,128)}, f32[2,7,1,128]{3,1,2,0:T(8,128)S(1)}, u32[]{:S(2)}, u32[]{:S(2)}) collective-permute-start(f32[2,7,1,128]{3,1,2,0:T(8,128)} %get-tuple-element.37), channel_id=1, source_target_pairs={{32,0},{64,32},{96,64},{128,96},{160,128},{192,160},{224,192},{33,... | collective-permute-start | bytes 21512 | tf_op jit(solution)/shard_map/ppermute | solution.py:53
  26.8 1.0 copy-start.8
  27.8 49.5 %copy-start.4 = (f32[6,128,128]{2,0,1:T(8,128)}, f32[6,128,128]{2,0,1:T(8,128)S(1)}, u32[]{:S(2)}) copy-start(f32[6,128,128]{2,0,1:T(8,128)S(1)} %copy.180) | copy-start | bytes 1179652
  32.8 11.0 %copy-start.9 = (f32[7]{0:T(128)S(1)}, f32[7]{0:T(128)}, u32[]{:S(2)}) copy-start(f32[7]{0:T(128)} %constant.10.clone) | copy-start | bytes 88
  36.5 15.3 %collective-permute-start.1 = (f32[2,7,1,128]{3,1,2,0:T(8,128)}, f32[2,7,1,128]{3,1,2,0:T(8,128)S(1)}, u32[]{:S(2)}, u32[]{:S(2)}) collective-permute-start(f32[2,7,1,128]{3,1,2,0:T(8,128)} %get-tuple-element.38), channel_id=1, source_target_pairs={{0,32},{32,64},{64,96},{96,128},{128,160},{160,192},{192,224},{1,3... | collective-permute-start | bytes 21512 | tf_op jit(solution)/shard_map/ppermute | solution.py:52
  38.5 16.7 %collective-permute-start.7 = (f32[2,7,128,1]{2,1,3,0:T(8,128)S(1)}, f32[2,7,128,1]{2,1,3,0:T(8,128)S(1)}, u32[]{:S(2)}, u32[]{:S(2)}) collective-permute-start(f32[2,7,128,1]{2,1,3,0:T(8,128)S(1)} %copy.211), channel_id=1, source_target_pairs={{1,0},{2,1},{3,2},{4,3},{5,4},{6,5},{7,6},{8,7},{9,8},{10,9},{11,1... | collective-permute-start | bytes 21512 | tf_op jit(solution)/shard_map/ppermute | solution.py:53
  39.8 14.0 %collective-permute-start.5 = (f32[2,7,128,1]{2,1,3,0:T(8,128)}, f32[2,7,128,1]{2,1,3,0:T(8,128)S(1)}, u32[]{:S(2)}, u32[]{:S(2)}) collective-permute-start(f32[2,7,128,1]{2,1,3,0:T(8,128)} %copy.210), channel_id=1, source_target_pairs={{0,1},{1,2},{2,3},{3,4},{4,5},{5,6},{6,7},{7,8},{8,9},{9,10},{10,1... | collective-permute-start | bytes 21512 | tf_op jit(solution)/shard_map/ppermute | solution.py:52
  46.2 11.0 %copy-start.1 = (f32[7,128,128]{2,0,1:T(8,128)}, f32[7,128,128]{2,0,1:T(8,128)S(1)}, u32[]{:S(2)}) copy-start(f32[7,128,128]{2,0,1:T(8,128)S(1)} %copy.183) | copy-start | bytes 1376260
  53.9 3.3 %copy-start.10 = (f32[7]{0:T(128)S(1)}, f32[7]{0:T(128)}, u32[]{:S(2)}) copy-start(f32[7]{0:T(128)} %constant.10.clone) | copy-start | bytes 88
  64.6 16.7 %collective-permute-start.8 = (f32[2,7,1,128]{3,1,2,0:T(8,128)S(1)}, f32[2,7,1,128]{3,1,2,0:T(8,128)S(1)}, u32[]{:S(2)}, u32[]{:S(2)}) collective-permute-start(f32[2,7,1,128]{3,1,2,0:T(8,128)S(1)} %get-tuple-element.35), channel_id=1, source_target_pairs={{0,32},{32,64},{64,96},{96,128},{128,160},{160,192},{192,224},{1,3... | collective-permute-start | bytes 21512 | tf_op jit(solution)/shard_map/ppermute | solution.py:52
  67.0 14.2 %collective-permute-start.9 = (f32[2,7,1,128]{3,1,2,0:T(8,128)S(1)}, f32[2,7,1,128]{3,1,2,0:T(8,128)S(1)}, u32[]{:S(2)}, u32[]{:S(2)}) collective-permute-start(f32[2,7,1,128]{3,1,2,0:T(8,128)S(1)} %get-tuple-element.36), channel_id=1, source_target_pairs={{32,0},{64,32},{96,64},{128,96},{160,128},{192,160},{224,192},{33,... | collective-permute-start | bytes 21512 | tf_op jit(solution)/shard_map/ppermute | solution.py:53
  72.1 7.8 %collective-permute-start.11 = (f32[2,7,128,1]{2,1,3,0:T(8,128)S(1)}, f32[2,7,128,1]{2,1,3,0:T(8,128)S(1)}, u32[]{:S(2)}, u32[]{:S(2)}) collective-permute-start(f32[2,7,128,1]{2,1,3,0:T(8,128)S(1)} %copy.186), channel_id=1, source_target_pairs={{1,0},{2,1},{3,2},{4,3},{5,4},{6,5},{7,6},{8,7},{9,8},{10,9},{11,1... | collective-permute-start | bytes 21512 | tf_op jit(solution)/shard_map/ppermute | solution.py:53
  73.4 5.1 %collective-permute-start.10 = (f32[2,7,128,1]{2,1,3,0:T(8,128)S(1)}, f32[2,7,128,1]{2,1,3,0:T(8,128)S(1)}, u32[]{:S(2)}, u32[]{:S(2)}) collective-permute-start(f32[2,7,128,1]{2,1,3,0:T(8,128)S(1)} %copy.184), channel_id=1, source_target_pairs={{0,1},{1,2},{2,3},{3,4},{4,5},{5,6},{6,7},{7,8},{8,9},{9,10},{10,1... | collective-permute-start | bytes 21512 | tf_op jit(solution)/shard_map/ppermute | solution.py:52
  78.5 2.7 %copy-start.5 = (f32[7,128,128]{2,0,1:T(8,128)S(1)}, f32[7,128,128]{2,0,1:T(8,128)}, u32[]{:S(2)}) copy-start(f32[7,128,128]{2,0,1:T(8,128)} %copy.163) | copy-start | bytes 1376260
  78.5 2.7 %copy-start.6 = (f32[7,128,128]{2,0,1:T(8,128)S(1)}, f32[7,128,128]{2,0,1:T(8,128)}, u32[]{:S(2)}) copy-start(f32[7,128,128]{2,0,1:T(8,128)} %copy.167) | copy-start | bytes 1376260
  125.2 18.0 %collective-permute-start.12 = (f32[2,7,1,128]{3,1,2,0:T(8,128)S(1)}, f32[2,7,1,128]{3,1,2,0:T(8,128)S(1)}, u32[]{:S(2)}, u32[]{:S(2)}) collective-permute-start(f32[2,7,1,128]{3,1,2,0:T(8,128)S(1)} %get-tuple-element.31), channel_id=1, source_target_pairs={{0,32},{32,64},{64,96},{96,128},{128,160},{160,192},{192,224},{1,3... | collective-permute-start | bytes 21512 | tf_op jit(solution)/shard_map/ppermute | solution.py:52
  128.0 15.2 %collective-permute-start.13 = (f32[2,7,1,128]{3,1,2,0:T(8,128)S(1)}, f32[2,7,1,128]{3,1,2,0:T(8,128)S(1)}, u32[]{:S(2)}, u32[]{:S(2)}) collective-permute-start(f32[2,7,1,128]{3,1,2,0:T(8,128)S(1)} %get-tuple-element.32), channel_id=1, source_target_pairs={{32,0},{64,32},{96,64},{128,96},{160,128},{192,160},{224,192},{33,... | collective-permute-start | bytes 21512 | tf_op jit(solution)/shard_map/ppermute | solution.py:53
  133.0 8.8 %collective-permute-start.15 = (f32[2,7,128,1]{2,1,3,0:T(8,128)S(1)}, f32[2,7,128,1]{2,1,3,0:T(8,128)S(1)}, u32[]{:S(2)}, u32[]{:S(2)}) collective-permute-start(f32[2,7,128,1]{2,1,3,0:T(8,128)S(1)} %copy.193), channel_id=1, source_target_pairs={{1,0},{2,1},{3,2},{4,3},{5,4},{6,5},{7,6},{8,7},{9,8},{10,9},{11,1... | collective-permute-start | bytes 21512 | tf_op jit(solution)/shard_map/ppermute | solution.py:53
  134.3 6.2 %collective-permute-start.14 = (f32[2,7,128,1]{2,1,3,0:T(8,128)S(1)}, f32[2,7,128,1]{2,1,3,0:T(8,128)S(1)}, u32[]{:S(2)}, u32[]{:S(2)}) collective-permute-start(f32[2,7,128,1]{2,1,3,0:T(8,128)S(1)} %copy.191), channel_id=1, source_target_pairs={{0,1},{1,2},{2,3},{3,4},{4,5},{5,6},{6,7},{7,8},{8,9},{9,10},{10,1... | collective-permute-start | bytes 21512 | tf_op jit(solution)/shard_map/ppermute | solution.py:52
  173.5 2.3 copy-start.2
  175.8 1.0 copy-start.7
  178.4 18.0 %collective-permute-start.16 = (f32[2,7,1,128]{3,1,2,0:T(8,128)S(1)}, f32[2,7,1,128]{3,1,2,0:T(8,128)S(1)}, u32[]{:S(2)}, u32[]{:S(2)}) collective-permute-start(f32[2,7,1,128]{3,1,2,0:T(8,128)S(1)} %get-tuple-element.27), channel_id=1, source_target_pairs={{0,32},{32,64},{64,96},{96,128},{128,160},{160,192},{192,224},{1,3... | collective-permute-start | bytes 21512 | tf_op jit(solution)/shard_map/ppermute | solution.py:52
  181.2 15.2 %collective-permute-start.17 = (f32[2,7,1,128]{3,1,2,0:T(8,128)S(1)}, f32[2,7,1,128]{3,1,2,0:T(8,128)S(1)}, u32[]{:S(2)}, u32[]{:S(2)}) collective-permute-start(f32[2,7,1,128]{3,1,2,0:T(8,128)S(1)} %get-tuple-element.28), channel_id=1, source_target_pairs={{32,0},{64,32},{96,64},{128,96},{160,128},{192,160},{224,192},{33,... | collective-permute-start | bytes 21512 | tf_op jit(solution)/shard_map/ppermute | solution.py:53
  186.2 8.8 %collective-permute-start.19 = (f32[2,7,128,1]{2,1,3,0:T(8,128)S(1)}, f32[2,7,128,1]{2,1,3,0:T(8,128)S(1)}, u32[]{:S(2)}, u32[]{:S(2)}) collective-permute-start(f32[2,7,128,1]{2,1,3,0:T(8,128)S(1)} %copy.199), channel_id=1, source_target_pairs={{1,0},{2,1},{3,2},{4,3},{5,4},{6,5},{7,6},{8,7},{9,8},{10,9},{11,1... | collective-permute-start | bytes 21512 | tf_op jit(solution)/shard_map/ppermute | solution.py:53
  187.5 6.2 %collective-permute-start.18 = (f32[2,7,128,1]{2,1,3,0:T(8,128)S(1)}, f32[2,7,128,1]{2,1,3,0:T(8,128)S(1)}, u32[]{:S(2)}, u32[]{:S(2)}) collective-permute-start(f32[2,7,128,1]{2,1,3,0:T(8,128)S(1)} %copy.197), channel_id=1, source_target_pairs={{0,1},{1,2},{2,3},{3,4},{4,5},{5,6},{6,7},{7,8},{8,9},{9,10},{10,1... | collective-permute-start | bytes 21512 | tf_op jit(solution)/shard_map/ppermute | solution.py:52
where the time goes:
time: 231 us; the launch traced here: 229 us
  blocking collectives  85.6 us (37%)
  starting transfers between devices  53.5 us (23%)
  local copies, waits for them, and re-layouts  52.2 us (23%)
  other arithmetic  37.2 us (16%)
    all_to_all x6, blocking collectives, sent_to_all(): return lax.all_to_all(copies, axis, split_axis=0, concat_axis=0, tiled=True)  85.6 us
    ppermute x10, starting transfers between devices, extended_2(): lax.ppermute(last, axis, up)  32.6 us
    ppermute x10, starting transfers between devices, extended_2(): lax.ppermute(leading, axis, [(b, a) for a, b in up])  20.8 us
    reduce_sum x4, other arithmetic, core_sum(): return jnp.sum(first * second, axis=(1, 2, 3))  15.9 us
    unnamed x44, local copies, waits for them, and re-layouts  13.3 us
    slice x10, local copies, waits for them, and re-layouts, extended_2(): last = lax.slice_in_dim(x, length - width, length, axis=dim)  10.9 us
    div x3, other arithmetic, per_device(): scaled = residual / diagonal  7.37 us
    slice x6, local copies, waits for them, and re-layouts, extended_2(): leading = lax.slice_in_dim(x, 0, width, axis=dim)  7 us
  transfers between devices with their start and end apart: 20, of which 0 were waited for; matrix products, arithmetic and copies ran while one was open for 23% of the time, Pallas kernels for 0%

commit v1 on v0

v1 whole, which is shorter than its diff:
```python
import functools

import jax
import jax.numpy as jnp
from jax import lax
from jax.experimental import pallas as pl
from jax.experimental.pallas import tpu as pltpu
from jax.sharding import PartitionSpec as P

TIER_K = (1.0, 0.3, 0.12, 2.5)
CHANNEL_K = (1.0, 0.3, 0.25, 0.2)
CHANNEL_SINK = (0.0, 0.15, 0.45, 1.2)
TIER_HEAT = 0.05
CHANNEL_HEAT = 0.2
VERTICAL = 4.0

SCEN, TIERS, LAYERS = 2, 4, 7
TILE = 128
HALO = 4
FIELDS = SCEN * LAYERS + SCEN * TIERS + LAYERS
DISS = SCEN * LAYERS
CODE = DISS + SCEN * TIERS
TOP = 16
ROWS = TOP + TILE + 16
F32 = jnp.float32


def tables(layer):
    if layer % 2 == 0:
        kappa, sink, heat = TIER_K, (0.0,) * 4, TIER_HEAT
    else:
        kappa, sink, heat = CHANNEL_K, CHANNEL_SINK, CHANNEL_HEAT
    root = [k**0.5 for k in kappa]
    return (
        (0.0, *root),
        (0.0, *[1.0 / r for r in root]),
        (1.0, *[(heat + s) / r for s, r in zip(sink, root)]),
        (0.0, *[s / r for s, r in zip(sink, root)]),
    )


def pick(code, table):
    out = jnp.full(code.shape, table[0], F32)
    for index in range(1, 5):
        out = jnp.where(code == float(index), F32(table[index]), out)
    return out


def code_of(material, coolant, layer, rows):
    block = material[layer // 2, rows] if layer % 2 == 0 else coolant[layer // 2, rows]
    return block.astype(F32) + 1.0


def field_rows(previous, dissipated, material, coolant, field, rows):
    if field < DISS:
        return previous[field // LAYERS, field % LAYERS, rows]
    if field < CODE:
        return dissipated[(field - DISS) // TIERS, (field - DISS) % TIERS, rows]
    return code_of(material, coolant, field - CODE, rows)


def pack_rows(pt, pb, dt, db, mt, mb, ct, cb, a_out, b_out):
    lower = lax.axis_index("gx") % 2 == 0
    for field in range(FIELDS):
        top = field_rows(pt, dt, mt, ct, field, slice(0, HALO))
        bottom = field_rows(pb, db, mb, cb, field, slice(8 - HALO, 8))
        rows = slice(HALO * field, HALO * (field + 1))
        a_out[rows, :] = jnp.where(lower, bottom, top)
        b_out[rows, :] = jnp.where(lower, top, bottom)


def pack_columns(prev, diss, mat, cool, a_in, b_in, halo_out, a_out, b_out):
    lower = lax.axis_index("gx") % 2 == 0
    west = lax.axis_index("gy") % 2 == 0
    for field in range(FIELDS):
        rows = slice(HALO * field, HALO * (field + 1))
        halo_out[field, :HALO, :] = jnp.where(lower, b_in[rows, :], a_in[rows, :])
        halo_out[field, HALO:, :] = jnp.where(lower, a_in[rows, :], b_in[rows, :])
    lane = lax.broadcasted_iota(jnp.int32, (8, TILE), 1)

    def pack(get, rows):
        low = jnp.zeros((8, TILE), F32)
        high = jnp.zeros((8, TILE), F32)
        for field in range(FIELDS):
            x = get(field)
            at = HALO * field
            mine = (lane >= at) & (lane < at + HALO)
            low = jnp.where(mine, pltpu.roll(x, at, 1) if at else x, low)
            high = jnp.where(mine, pltpu.roll(x, at + HALO, 1), high)
        a_out[rows, :] = jnp.where(west, high, low)
        b_out[rows, :] = jnp.where(west, low, high)

    @pl.loop(0, TILE // 8)
    def _(k):
        rows = pl.ds(pl.multiple_of(8 * k, 8), 8)
        pack(lambda field: field_rows(prev, diss, mat, cool, field, rows), rows)

    pack(lambda field: halo_out[field], slice(TILE, TILE + 8))


def solve(prev, diss, mat, cool, halo, a_in, b_in, w0_out, w1_out, w2_out, m_out,
          sa, sb, ypa, ypb, xb, qa, qb, y0a, y0b, y1a, y1b, y2a, y2b):
    west = lax.axis_index("gy") % 2 == 0
    lane = lax.broadcasted_iota(jnp.int32, (8, TILE), 1)
    first, last = lane == 0, lane == TILE - 1
    zero = jnp.zeros((8, TILE), F32)

    def start(get, get_code, message_rows, stores):
        a, b = a_in[message_rows, :], b_in[message_rows, :]
        east = jnp.where(west, a, b)
        wst = jnp.where(west, b, a)

        def strip(field):
            at = HALO * field
            x = jnp.where(lane < HALO, pltpu.roll(east, (TILE - at) % TILE, 1) if at else east, zero)
            return jnp.where(lane >= TILE - HALO, pltpu.roll(wst, (2 * TILE - HALO - at) % TILE, 1), x)

        def put(ref, index, value):
            for rows, shift in stores:
                ref[index, rows, :] = pltpu.roll(value, shift, 0) if shift else value

        for layer in range(LAYERS):
            root = tables(layer)[0]
            s = pick(get_code(layer), root)
            put(sa, layer, s)
            c = strip(CODE + layer)
            put(xb, CODE + layer, c)
            s2 = pick(c, root)
            put(sb, layer, s2)
            for scen in range(SCEN):
                f = scen * LAYERS + layer
                put(ypa, f, s * get(f))
                x = strip(f)
                put(xb, f, x)
                put(ypb, f, s2 * x)
                if layer % 2 == 0:
                    d = DISS + scen * TIERS + layer // 2
                    put(xb, d, strip(d))

    @pl.loop(0, TILE // 8)
    def _(k):
        rows = pl.ds(pl.multiple_of(8 * k, 8), 8)
        start(
            lambda f: field_rows(prev, diss, mat, cool, f, rows),
            lambda layer: code_of(mat, cool, layer, rows),
            rows,
            ((pl.ds(pl.multiple_of(8 * k + TOP, 8), 8), 0),),
        )

    start(
        lambda f: halo[f],
        lambda layer: halo[CODE + layer],
        slice(TILE, TILE + 8),
        ((slice(TOP - 8, TOP), 4), (slice(TOP + TILE, TOP + TILE + 8), 4)),
    )

    def around(xa, xb_, base, r, both):
        here = pl.ds(r, 8)
        a = [xa[base + layer, here, :] for layer in range(LAYERS)]
        b = [xb_[base + layer, here, :] for layer in range(LAYERS)]
        out_a, out_b = [], []
        for layer in range(LAYERS):
            down_a, down_b = pltpu.roll(a[layer], 1, 1), pltpu.roll(b[layer], 1, 1)
            up_a, up_b = pltpu.roll(a[layer], TILE - 1, 1), pltpu.roll(b[layer], TILE - 1, 1)

            def total(x, x_ref, to_west, to_east):
                f = base + layer
                t = (x_ref[f, pl.ds(r - 1, 8), :] + x_ref[f, pl.ds(r + 1, 8), :]) + (to_west + to_east)
                if layer == 0:
                    return t + VERTICAL * x[1]
                if layer == LAYERS - 1:
                    return t + VERTICAL * x[layer - 1]
                return t + VERTICAL * (x[layer - 1] + x[layer + 1])

            out_a.append(total(a, xa, jnp.where(first, down_b, down_a), jnp.where(last, up_b, up_a)))
            if both:
                out_b.append(total(b, xb_, jnp.where(first, down_a, down_b), jnp.where(last, up_a, up_b)))
        return a, b, out_a, out_b

    def tree(terms):
        while len(terms) > 1:
            terms = [sum(terms[i : i + 2][1:], terms[i]) for i in range(0, len(terms), 2)]
        return terms[0]

    def first_step(r, main, get, get_code):
        here = pl.ds(r, 8)
        _, _, ssa, ssb = around(sa, sb, 0, r, True)
        q_a, q_b = [], []
        for layer in range(LAYERS):
            _, _, over, _ = tables(layer)
            s, s2 = sa[layer, here, :], sb[layer, here, :]
            q_a.append(s / (pick(get_code(layer), over) + ssa[layer]))
            q_b.append(s2 / (pick(xb[CODE + layer, here, :], over) + ssb[layer]))
            qa[layer, here, :] = q_a[-1]
            qb[layer, here, :] = q_b[-1]
        sums = []
        for scen in range(SCEN):
            base = scen * LAYERS
            _, _, ta, tb = around(ypa, ypb, base, r, True)
            products = []
            for layer in range(LAYERS):
                _, inverse, _, loss = tables(layer)
                f = base + layer
                d = DISS + scen * TIERS + layer // 2
                code, code2 = get_code(layer), xb[CODE + layer, here, :]
                t = ta[layer] - (pick(code, loss) + ssa[layer]) * get(f)
                t2 = tb[layer] - (pick(code2, loss) + ssb[layer]) * xb[f, here, :]
                if layer % 2 == 0:
                    t = t + get(d) * pick(code, inverse)
                    t2 = t2 + xb[d, here, :] * pick(code2, inverse)
                y = q_a[layer] * t
                y0a[f, here, :] = y
                y0b[f, here, :] = q_b[layer] * t2
                products.append(y * t)
            sums.append(tree(products))
        return tuple(sums) if main else None

    def main_first(k, acc):
        rows = pl.ds(pl.multiple_of(8 * k, 8), 8)
        sums = first_step(
            pl.multiple_of(8 * k + TOP, 8),
            True,
            lambda f: field_rows(prev, diss, mat, cool, f, rows),
            lambda layer: code_of(mat, cool, layer, rows),
        )
        return tuple(a + s for a, s in zip(acc, sums))

    none = (zero,) * SCEN
    m0 = lax.fori_loop(0, TILE // 8, main_first, none)
    for r in (TOP - 8, TOP + TILE):
        first_step(r, False, lambda f: pltpu.roll(halo[f], 4, 0), lambda layer: pltpu.roll(halo[CODE + layer], 4, 0))

    def step(xa, xb_, na, nb, r):
        here = pl.ds(r, 8)
        odd, even = [], []
        for scen in range(SCEN):
            base = scen * LAYERS
            a, _, ta, tb = around(xa, xb_, base, r, True)
            p, p2 = [], []
            for layer in range(LAYERS):
                f = base + layer
                y = qa[layer, here, :] * ta[layer]
                na[f, here, :] = y
                nb[f, here, :] = qb[layer, here, :] * tb[layer]
                p.append(a[layer] * ta[layer])
                p2.append(y * ta[layer])
            odd.append(tree(p))
            even.append(tree(p2))
        return (*odd, *even)

    def sweep(xa, xb_, na, nb):
        def body(k, acc):
            return tuple(a + s for a, s in zip(acc, step(xa, xb_, na, nb, pl.multiple_of(8 * k + TOP, 8))))

        acc = lax.fori_loop(0, TILE // 8, body, none + none)
        for r in (TOP - 8, TOP + TILE):
            step(xa, xb_, na, nb, r)
        return acc[:SCEN], acc[SCEN:]

    m1, m2 = sweep(y0a, y0b, y1a, y1b)
    m3, m4 = sweep(y1a, y1b, y2a, y2b)

    def final(k, acc):
        rows = pl.ds(pl.multiple_of(8 * k, 8), 8)
        r = pl.multiple_of(8 * k + TOP, 8)
        here = pl.ds(r, 8)
        scale = [pick(code_of(mat, cool, layer, rows), tables(layer)[1]) for layer in range(LAYERS)]
        sums = []
        for scen in range(SCEN):
            base = scen * LAYERS
            a, _, ta, _ = around(y2a, y2b, base, r, False)
            sums.append(tree([a[layer] * ta[layer] for layer in range(LAYERS)]))
            for layer in range(LAYERS):
                f = base + layer
                w2_out[f, rows, :] = scale[layer] * a[layer]
                w1_out[f, rows, :] = scale[layer] * y1a[f, here, :]
                w0_out[f, rows, :] = scale[layer] * y0a[f, here, :]
        return tuple(x + s for x, s in zip(acc, sums))

    m5 = lax.fori_loop(0, TILE // 8, final, none)
    line = lax.broadcasted_iota(jnp.int32, (1, TILE), 1)
    out = jnp.zeros((1, TILE), F32)
    for index, moment in enumerate((m0, m1, m2, m3, m4, m5)):
        for scen in range(SCEN):
            value = jnp.sum(jnp.sum(moment[scen], axis=0, keepdims=True), axis=1, keepdims=True)
            out = jnp.where(line == SCEN * index + scen, value, out)
    m_out[...] = out


def swaps(devices):
    near = [(i, i ^ 1) for i in range(devices)]
    far = [(i, i + 1) for i in range(1, devices - 1, 2)]
    return near, far + [(b, a) for a, b in far]


def exchange(a, b, axis):
    near, far = swaps(lax.axis_size(axis))
    return lax.ppermute(a, axis, near), lax.ppermute(b, axis, far)


def coefficients(m):
    h11, h12, h13, h23, h33 = (m[i] - m[i + 1] for i in range(5))
    h22 = h13

    def inverse(x):
        return jnp.where(x > 0, 1.0 / jnp.where(x > 0, x, 1.0), 0.0)

    d1 = inverse(h11)
    l21, l31 = h12 * d1, h13 * d1
    d2 = inverse(h22 - l21 * h12)
    u23 = h23 - l31 * h12
    l32 = u23 * d2
    d3 = inverse(h33 - l31 * h13 - l32 * u23)
    g1 = m[0]
    g2 = m[1] - l21 * g1
    g3 = m[2] - l31 * g1 - l32 * g2
    c3 = g3 * d3
    c2 = g2 * d2 - l32 * c3
    c1 = g1 * d1 - l21 * c2 - l31 * c3
    return c1, c2, c3


def vmem(n):
    return [pl.BlockSpec(memory_space=pltpu.VMEM)] * n


def shape(*dims):
    return jax.ShapeDtypeStruct(dims, F32)


def params(mib):
    return pltpu.CompilerParams(vmem_limit_bytes=mib << 20)


def per_device(previous, dissipated, material, coolant):
    lasts = TILE // 8 - 1
    edge_specs = []
    for a in (previous, dissipated, material, coolant):
        for at in (0, lasts):
            block = (*a.shape[:-2], 8, TILE)
            edge_specs.append(pl.BlockSpec(block, functools.partial(lambda n, at, i: (0,) * n + (at, 0), a.ndim - 2, at)))
    a, b = pl.pallas_call(
        pack_rows,
        grid=(1,),
        in_specs=edge_specs,
        out_specs=[pl.BlockSpec((FIELDS * HALO, TILE), lambda i: (0, 0))] * 2,
        out_shape=[shape(FIELDS * HALO, TILE)] * 2,
        compiler_params=params(8),
    )(previous, previous, dissipated, dissipated, material, material, coolant, coolant)
    a, b = exchange(a, b, "gx")
    halo, a, b = pl.pallas_call(
        pack_columns,
        in_specs=vmem(6),
        out_specs=vmem(3),
        out_shape=[shape(FIELDS, 8, TILE)] + [shape(TILE + 8, TILE)] * 2,
        compiler_params=params(16),
    )(previous, dissipated, material, coolant, a, b)
    a, b = exchange(a, b, "gy")

    def padded(fields):
        return pltpu.VMEM((fields, ROWS, TILE), F32)

    pairs = SCEN * LAYERS
    w0, w1, w2, moments = pl.pallas_call(
        solve,
        in_specs=vmem(7),
        out_specs=vmem(4),
        out_shape=[shape(pairs, TILE, TILE)] * 3 + [shape(1, TILE)],
        scratch_shapes=[padded(LAYERS)] * 2
        + [padded(pairs)] * 2
        + [padded(FIELDS)]
        + [padded(LAYERS)] * 2
        + [padded(pairs)] * 6,
        compiler_params=params(40),
    )(previous, dissipated, material, coolant, halo, a, b)
    devices = lax.axis_size("gx") * lax.axis_size("gy")
    copies = jnp.broadcast_to(moments, (devices, 1, TILE))
    everything = lax.all_to_all(copies, ("gx", "gy"), split_axis=0, concat_axis=0, tiled=True)
    total = jnp.sum(everything, axis=(0, 1))
    c = coefficients([total[SCEN * i : SCEN * (i + 1)] for i in range(6)])
    c = [x[:, None, None, None] for x in c]
    w0, w1, w2 = (w.reshape(previous.shape) for w in (w0, w1, w2))
    return previous + (c[0] * w0 + c[1] * w1 + c[2] * w2)


def solution(mesh):
    placed = (P(None, None, "gx", "gy"),) * 2 + (P(None, "gx", "gy"),) * 2
    return jax.shard_map(
        per_device, mesh=mesh, in_specs=placed, out_specs=P(None, None, "gx", "gy"), check_vma=False
    )
```

time: 231 us -> 65.6 us (0.28)
  blocking collectives: 85.6 us -> 30.7 us
  starting transfers between devices: 53.5 us -> 5.95 us
  local copies, waits for them, and re-layouts: 52.2 us -> 5.1 us
  other arithmetic: 37.2 us -> 2.65 us
  Pallas kernels: 0 us -> 14.6 us
  waiting for transfers between devices: 0.05 us -> 6.08 us
    all_to_all x6 -> x1, blocking collectives: 85.6 us -> 30.7 us  [per_device(): lax.all_to_all(copies, ('gx', 'gy'), split_axis=0, concat_axis=0, tiled=T...]
    ppermute x20 -> x4, starting transfers between devices: 53.5 us -> 5.95 us  [exchange(): return (lax.ppermute(a, axis, near), lax.ppermute(b, axis, far))]
    slice x17 -> x0, local copies, waits for them, and re-layouts: 18.7 us -> none  [the longest x10 10.9 us: extended_2(): last = lax.slice_in_dim(x, length - width, length, axis=dim)]
    reduce_sum x10 -> x1, other arithmetic: 16.1 us -> 0.05 us  [per_device(): total = jnp.sum(everything, axis=(0, 1))]
    pallas_call x0 -> x3, Pallas kernels: none -> 14.6 us  [the longest x1 12.4 us: per_device(): pl.pallas_call(solve, in_specs=vmem(7), out_specs=vmem(4), out_shape=[sha...]
    unnamed x44 -> x18, local copies, waits for them, and re-layouts: 13.3 us -> 5.03 us
    ppermute x6 -> x0, local copies, waits for them, and re-layouts: 8.17 us -> none  [the longest x3 4.09 us: extended_2(): lax.ppermute(last, axis, up)]
    div x6 -> x0, other arithmetic: 7.6 us -> none  [the longest x3 7.37 us: per_device(): scaled = residual / diagonal]
  transfers between devices with their start and end apart: 20 -> 4, of which waited for: 0 -> 2; matrix products, arithmetic and copies ran while one was open for 23% -> 0% of each run, Pallas kernels for 0% -> 0%
where the time goes in v1:
time: 65.6 us; the launch traced here: 65.3 us
  blocking collectives  30.7 us (47%)
  Pallas kernels  14.6 us (22%)
  waiting for transfers between devices  6.08 us (9%)
  starting transfers between devices  5.95 us (9%)
  local copies, waits for them, and re-layouts  5.1 us (8%)
  other arithmetic  2.65 us (4%)
    all_to_all x1, blocking collectives, per_device(): lax.all_to_all(copies, ('gx', 'gy'), split_axis=0, concat_axis=0, tiled=T...  30.7 us
    pallas_call x1, Pallas kernels, per_device(): pl.pallas_call(solve, in_specs=vmem(7), out_specs=vmem(4), out_shape=[sha...  12.4 us
    ppermute x4, waiting for transfers between devices, exchange(): return (lax.ppermute(a, axis, near), lax.ppermute(b, axis, far))  6.08 us
    ppermute x4, starting transfers between devices, exchange(): return (lax.ppermute(a, axis, near), lax.ppermute(b, axis, far))  5.95 us
    unnamed x18, local copies, waits for them, and re-layouts  5.03 us
    add x1, other arithmetic, per_device(): return previous + (c[0] * w0 + c[1] * w1 + c[2] * w2)  2.43 us
    pallas_call x1, Pallas kernels, per_device(): pl.pallas_call(pack_columns, in_specs=vmem(6), out_specs=vmem(3), out_sha...  2.21 us
  transfers between devices with their start and end apart: 4, of which 2 were waited for; matrix products, arithmetic and copies ran while one was open for 0% of the time, Pallas kernels for 0%

profile of v1, /device:TPU:1, one launch (start us, length us, event | category | flops | bytes accessed | tf_op | source)
XLA Modules:
  0.0 65.3 jit_solution(12385420951808476411)
XLA Ops:
  0.0 0.0 copy-start
  0.0 1.2 %copy-done = f32[2,7,128,128]{3,2,1,0:T(8,128)S(1)} copy-done((f32[2,7,128,128]{3,2,1,0:T(8,128)S(1)}, f32[2,7,128,128]{3,2,1,0:T(8,128)}, u32[]{:S(2)}) %copy-start) | copy-done | bytes 917528
  1.2 0.0 copy-start.2
  1.2 1.0 %copy-done.2 = f32[2,4,128,128]{3,2,1,0:T(8,128)S(1)} copy-done((f32[2,4,128,128]{3,2,1,0:T(8,128)S(1)}, f32[2,4,128,128]{3,2,1,0:T(8,128)}, u32[]{:S(2)}) %copy-start.2) | copy-done | bytes 524312
  2.2 0.0 copy-start.4
  2.2 0.9 %copy-done.4 = s32[4,128,128]{2,1,0:T(8,128)S(1)} copy-done((s32[4,128,128]{2,1,0:T(8,128)S(1)}, s32[4,128,128]{2,1,0:T(8,128)}, u32[]{:S(2)}) %copy-start.4) | copy-done | bytes 262168
  3.2 0.0 copy-start.6
  3.2 0.9 %copy-done.6 = s32[3,128,128]{2,1,0:T(8,128)S(1)} copy-done((s32[3,128,128]{2,1,0:T(8,128)S(1)}, s32[3,128,128]{2,1,0:T(8,128)}, u32[]{:S(2)}) %copy-start.6) | copy-done | bytes 196632
  4.1 0.0 copy-start.1
  4.1 0.0 copy-start.3
  4.1 0.0 copy-start.5
  4.1 0.0 copy-start.7
  4.2 3.3 %collective-permute-start = (f32[116,128]{1,0:T(8,128)S(1)}, f32[116,128]{1,0:T(8,128)S(1)}, u32[]{:S(2)}, u32[]{:S(2)}) collective-permute-start(f32[116,128]{1,0:T(8,128)S(1)} %get-tuple-element.14), channel_id=1, source_target_pairs={{0,32},{32,0},{64,96},{96,64},{128,160},{160,128},{192,224},{224,1... | collective-permute-start | bytes 178184 | tf_op jit(solution)/shard_map/ppermute | solution.py:298
  7.4 1.9 %collective-permute-start.1 = (f32[116,128]{1,0:T(8,128)S(1)}, f32[116,128]{1,0:T(8,128)S(1)}, u32[]{:S(2)}, u32[]{:S(2)}) collective-permute-start(f32[116,128]{1,0:T(8,128)S(1)} %get-tuple-element.15), channel_id=1, source_target_pairs={{32,64},{96,128},{160,192},{64,32},{128,96},{192,160},{33,65},{97,... | collective-permute-start | bytes 178184 | tf_op jit(solution)/shard_map/ppermute | solution.py:298
  9.4 0.0 collective-permute-done.a_in
  9.4 3.6 %collective-permute-done.1.b_in = f32[116,128]{1,0:T(8,128)S(1)} collective-permute-done((f32[116,128]{1,0:T(8,128)S(1)}, f32[116,128]{1,0:T(8,128)S(1)}, u32[]{:S(2)}, u32[]{:S(2)}) %collective-permute-start.1) | collective-permute-done | bytes 59424 | tf_op jit(solution)/shard_map/ppermute | solution.py:298
  13.0 0.0 copy-done.1
  13.0 0.0 copy-done.3
  13.0 0.0 copy-done.5
  13.0 0.0 copy-done.7
  13.0 2.2 %shard_map.47 = (f32[29,8,128]{2,1,0:T(8,128)S(1)}, f32[136,128]{1,0:T(8,128)S(1)}, f32[136,128]{1,0:T(8,128)S(1)}) custom-call(f32[2,7,128,128]{3,2,1,0:T(8,128)S(1)} %copy-done.1, f32[2,4,128,128]{3,2,1,0:T(8,128)S(1)} %copy-done.3, s32[4,128,128]{2,1,0:T(8,128)S(1)} %copy-done.5, s32[3,128,128]{2,1,0:T(8,128)S(1)} %copy-done.7, ...), custom_call_target="tpu_custom_call" | custom-call | tf_op jit(solution)/shard_map/pallas_call | solution.py:351
  15.2 0.1 collective-permute-start.2
  15.3 0.7 %collective-permute-start.3 = (f32[136,128]{1,0:T(8,128)S(1)}, f32[136,128]{1,0:T(8,128)S(1)}, u32[]{:S(2)}, u32[]{:S(2)}) collective-permute-start(f32[136,128]{1,0:T(8,128)S(1)} %get-tuple-element.18), channel_id=1, source_target_pairs={{1,2},{3,4},{5,6},{7,8},{9,10},{11,12},{13,14},{15,16},{17,18},{19... | collective-permute-start | bytes 208904 | tf_op jit(solution)/shard_map/ppermute | solution.py:298
  16.0 2.5 %collective-permute-done.2.a_in = f32[136,128]{1,0:T(8,128)S(1)} collective-permute-done((f32[136,128]{1,0:T(8,128)S(1)}, f32[136,128]{1,0:T(8,128)S(1)}, u32[]{:S(2)}, u32[]{:S(2)}) %collective-permute-start.2) | collective-permute-done | bytes 69664 | tf_op jit(solution)/shard_map/ppermute | solution.py:298
  18.5 0.0 collective-permute-done.3.b_in
  18.5 12.4 %shard_map.48 = (f32[14,128,128]{2,1,0:T(8,128)S(1)}, f32[14,128,128]{2,1,0:T(8,128)S(1)}, f32[14,128,128]{2,1,0:T(8,128)S(1)}, f32[1,128]{1,0:T(1,128)S(1)}) custom-call(f32[2,7,128,128]{3,2,1,0:T(8,128)S(1)} %copy-done.1, f32[2,4,128,128]{3,2,1,0:T(8,128)S(1)} %copy-done.3, s32[4,128,128]{2,1,0:T(8,128)S(1)} %copy-done.5, s32[3,128,128]{2,1,0:T(8,128)S(1)} %copy-done.7, ...), custom_call_target="tpu_custom_call" | custom-call | tf_op jit(solution)/shard_map/pallas_call | solution.py:364
  30.9 0.0 copy-start.8
  30.9 0.9 %copy-done.8 = f32[14,128,128]{2,1,0:T(8,128)} copy-done((f32[14,128,128]{2,1,0:T(8,128)}, f32[14,128,128]{2,1,0:T(8,128)S(1)}, u32[]{:S(2)}) %copy-start.8) | copy-done | bytes 917528
  31.8 0.1 broadcast_in_dim.13
  31.9 30.7 %all_to_all.5 = f32[256,1,128]{2,1,0:T(1,128)S(1)} all-to-all(f32[256,1,128]{2,1,0:T(1,128)S(1)} %broadcast_in_dim.13), channel_id=1, replica_groups=mesh['gx'=8,'gy'=32] {'gx','gy'}, dimensions={0} | all-to-all | bytes 262144 | tf_op jit(solution)/shard_map/all_to_all | solution.py:378
  62.6 0.1 fusion.4
  62.7 0.1 multiply_subtract_fusion
  62.8 2.4 %add_add_fusion = f32[2,7,128,128]{3,2,1,0:T(8,128)} fusion(f32[2,7,128,128]{3,2,1,0:T(8,128)S(1)} %copy-done.1, f32[2,7,128,128]{3,2,1,0:T(8,128)} %bitcast.7, f32[2,7,128,128]{3,2,1,0:T(8,128)S(1)} %bitcast.6, f32[2,7,128,128]{3,2,1,0:T(8,128)S(1)} %bitcast.5, f32[2]{0:T(128)S(1)} %get-tuple-element.25, f32[2]{0:T(128)S(1)} %get-tuple-element.24, ...), kind=kLoop, calls=%fused_computation | loop fusion | flops 1376256 | bytes 4587544 | tf_op jit(solution)/shard_map/add | solution.py:383
  (2 shorter events, 0.1 us)
Async XLA Ops:
  0.0 1.2 %copy-start = (f32[2,7,128,128]{3,2,1,0:T(8,128)S(1)}, f32[2,7,128,128]{3,2,1,0:T(8,128)}, u32[]{:S(2)}) copy-start(f32[2,7,128,128]{3,2,1,0:T(8,128)} %prev.3) | copy-start | bytes 2752516
  1.2 1.0 %copy-start.2 = (f32[2,4,128,128]{3,2,1,0:T(8,128)S(1)}, f32[2,4,128,128]{3,2,1,0:T(8,128)}, u32[]{:S(2)}) copy-start(f32[2,4,128,128]{3,2,1,0:T(8,128)} %diss.3) | copy-start | bytes 1572868
  2.2 0.9 %copy-start.4 = (s32[4,128,128]{2,1,0:T(8,128)S(1)}, s32[4,128,128]{2,1,0:T(8,128)}, u32[]{:S(2)}) copy-start(s32[4,128,128]{2,1,0:T(8,128)} %mat.3) | copy-start | bytes 786436
  3.2 0.9 %copy-start.6 = (s32[3,128,128]{2,1,0:T(8,128)S(1)}, s32[3,128,128]{2,1,0:T(8,128)}, u32[]{:S(2)}) copy-start(s32[3,128,128]{2,1,0:T(8,128)} %cool.3) | copy-start | bytes 589828
  4.1 8.9 %copy-start.1 = (f32[2,7,128,128]{3,2,1,0:T(8,128)S(1)}, f32[2,7,128,128]{3,2,1,0:T(8,128)}, u32[]{:S(2)}) copy-start(f32[2,7,128,128]{3,2,1,0:T(8,128)} %prev.3) | copy-start | bytes 2752516
  4.1 8.9 %copy-start.3 = (f32[2,4,128,128]{3,2,1,0:T(8,128)S(1)}, f32[2,4,128,128]{3,2,1,0:T(8,128)}, u32[]{:S(2)}) copy-start(f32[2,4,128,128]{3,2,1,0:T(8,128)} %diss.3) | copy-start | bytes 1572868
  4.1 8.9 %copy-start.5 = (s32[4,128,128]{2,1,0:T(8,128)S(1)}, s32[4,128,128]{2,1,0:T(8,128)}, u32[]{:S(2)}) copy-start(s32[4,128,128]{2,1,0:T(8,128)} %mat.3) | copy-start | bytes 786436
  4.1 8.9 %copy-start.7 = (s32[3,128,128]{2,1,0:T(8,128)S(1)}, s32[3,128,128]{2,1,0:T(8,128)}, u32[]{:S(2)}) copy-start(s32[3,128,128]{2,1,0:T(8,128)} %cool.3) | copy-start | bytes 589828
  4.2 5.2 %collective-permute-start = (f32[116,128]{1,0:T(8,128)S(1)}, f32[116,128]{1,0:T(8,128)S(1)}, u32[]{:S(2)}, u32[]{:S(2)}) collective-permute-start(f32[116,128]{1,0:T(8,128)S(1)} %get-tuple-element.14), channel_id=1, source_target_pairs={{0,32},{32,0},{64,96},{96,64},{128,160},{160,128},{192,224},{224,1... | collective-permute-start | bytes 178184 | tf_op jit(solution)/shard_map/ppermute | solution.py:298
  7.4 5.5 %collective-permute-start.1 = (f32[116,128]{1,0:T(8,128)S(1)}, f32[116,128]{1,0:T(8,128)S(1)}, u32[]{:S(2)}, u32[]{:S(2)}) collective-permute-start(f32[116,128]{1,0:T(8,128)S(1)} %get-tuple-element.15), channel_id=1, source_target_pairs={{32,64},{96,128},{160,192},{64,32},{128,96},{192,160},{33,65},{97,... | collective-permute-start | bytes 178184 | tf_op jit(solution)/shard_map/ppermute | solution.py:298
  15.2 3.2 %collective-permute-start.2 = (f32[136,128]{1,0:T(8,128)S(1)}, f32[136,128]{1,0:T(8,128)S(1)}, u32[]{:S(2)}, u32[]{:S(2)}) collective-permute-start(f32[136,128]{1,0:T(8,128)S(1)} %get-tuple-element.17), channel_id=1, source_target_pairs={{0,1},{1,0},{2,3},{3,2},{4,5},{5,4},{6,7},{7,6},{8,9},{9,8},{10,11... | collective-permute-start | bytes 208904 | tf_op jit(solution)/shard_map/ppermute | solution.py:298
  15.3 3.1 %collective-permute-start.3 = (f32[136,128]{1,0:T(8,128)S(1)}, f32[136,128]{1,0:T(8,128)S(1)}, u32[]{:S(2)}, u32[]{:S(2)}) collective-permute-start(f32[136,128]{1,0:T(8,128)S(1)} %get-tuple-element.18), channel_id=1, source_target_pairs={{1,2},{3,4},{5,6},{7,8},{9,10},{11,12},{13,14},{15,16},{17,18},{19... | collective-permute-start | bytes 208904 | tf_op jit(solution)/shard_map/ppermute | solution.py:298
  30.9 0.9 %copy-start.8 = (f32[14,128,128]{2,1,0:T(8,128)}, f32[14,128,128]{2,1,0:T(8,128)S(1)}, u32[]{:S(2)}) copy-start(f32[14,128,128]{2,1,0:T(8,128)S(1)} %get-tuple-element.22) | copy-start | bytes 2752516

commit v2 on v0

v2 whole, which is shorter than its diff:
```python
import functools

import jax
import jax.numpy as jnp
from jax import lax
from jax.experimental import pallas as pl
from jax.experimental.pallas import tpu as pltpu
from jax.sharding import PartitionSpec as P

TIER_K = (1.0, 0.3, 0.12, 2.5)
CHANNEL_K = (1.0, 0.3, 0.25, 0.2)
CHANNEL_SINK = (0.0, 0.15, 0.45, 1.2)
TIER_HEAT = 0.05
CHANNEL_HEAT = 0.2
VERTICAL = 4.0

SCEN, TIERS, LAYERS = 2, 4, 7
PAIRS = SCEN * LAYERS
TILE = 128
HALO = 4
GROUP = 16
CHUNKS = TILE // 8
FIELDS = PAIRS + SCEN * TIERS + LAYERS
DISS = PAIRS
CODE = DISS + SCEN * TIERS
MOMENTS = 6
F32 = jnp.float32
ROOT, INVERSE, OVER, LOSS = range(4)


def tables(tier):
    if tier:
        kappa, sink, heat = TIER_K, (0.0,) * 4, TIER_HEAT
    else:
        kappa, sink, heat = CHANNEL_K, CHANNEL_SINK, CHANNEL_HEAT
    root = [k**0.5 for k in kappa]
    return (
        (0.0, *root),
        (0.0, *[1.0 / r for r in root]),
        (1.0, *[(heat + s) / r for s, r in zip(sink, root)]),
        (0.0, *[s / r for s, r in zip(sink, root)]),
    )


def pick(code, table):
    out = jnp.full(code.shape, table[0], F32)
    for index in range(1, 5):
        if table[index] != table[0]:
            out = jnp.where(code == float(index), F32(table[index]), out)
    return out


def pick_inside(code, table):
    out = jnp.full(code.shape, table[4], F32)
    for index in range(1, 4):
        if table[index] != table[4]:
            out = jnp.where(code == float(index), F32(table[index]), out)
    return out


def turn(x, shift, axis=1):
    shift %= x.shape[axis]
    return pltpu.roll(x, shift, axis) if shift else x


def tree(terms):
    while len(terms) > 1:
        terms = [terms[i] + terms[i + 1] if i + 1 < len(terms) else terms[i] for i in range(0, len(terms), 2)]
    return terms[0]


def field_rows(previous, dissipated, material, coolant, field, rows):
    if field < DISS:
        return previous[field // LAYERS, field % LAYERS, rows]
    if field < CODE:
        return dissipated[(field - DISS) // TIERS, (field - DISS) % TIERS, rows]
    layer = field - CODE
    block = material[layer // 2, rows] if layer % 2 == 0 else coolant[layer // 2, rows]
    return block.astype(F32) + 1.0


def pack_rows(prev, diss, mat, cool, a_out, b_out, pt, pb, dt, db, mt, mb, ct, cb, sems):
    copies = []
    for index, (source, top, bottom) in enumerate(((prev, pt, pb), (diss, dt, db), (mat, mt, mb), (cool, ct, cb))):
        lead = (slice(None),) * (len(source.shape) - 2)
        for side, (target, at) in enumerate(((top, 0), (bottom, TILE - 8))):
            copies.append(pltpu.make_async_copy(source.at[(*lead, pl.ds(at, 8))], target, sems.at[2 * index + side]))
    for copy in copies:
        copy.start()
    lower = lax.axis_index("gx") % 2 == 0
    for copy in copies:
        copy.wait()
    for field in range(FIELDS):
        top = field_rows(pt, dt, mt, ct, field, slice(0, HALO))
        bottom = field_rows(pb, db, mb, cb, field, slice(8 - HALO, 8))
        rows = slice(HALO * field, HALO * (field + 1))
        a_out[rows, :] = jnp.where(lower, bottom, top)
        b_out[rows, :] = jnp.where(lower, top, bottom)


def strips_of(get, lane):
    zero = jnp.zeros((8, TILE), F32)
    blocks = []
    for fields in (
        [(layer, layer) for layer in range(LAYERS)],
        [(layer, LAYERS + layer) for layer in range(LAYERS)],
        [(layer, CODE + layer) for layer in range(LAYERS)],
        [(2 * t, DISS + t) for t in range(TIERS)],
        [(2 * t, DISS + TIERS + t) for t in range(TIERS)],
    ):
        out = zero
        for layer, field in fields:
            out = jnp.where(lane // GROUP == layer, turn(get(field), GROUP * layer + 8), out)
        blocks.append(out)
    return blocks


def neighbours(ref, base, r, x):
    out = []
    for layer in range(LAYERS):
        f = base + layer
        t = (ref[f, pl.ds(r - 1, 8), :] + ref[f, pl.ds(r + 1, 8), :]) + (turn(x[layer], 1) + turn(x[layer], -1))
        if layer == 0:
            t = t + VERTICAL * x[1]
        elif layer == LAYERS - 1:
            t = t + VERTICAL * x[layer - 1]
        else:
            t = t + VERTICAL * (x[layer - 1] + x[layer + 1])
        out.append(t)
    return out


def rows_of(ref, base, r, count=LAYERS):
    return [ref[base + i, pl.ds(r, 8), :] for i in range(count)]


def start_field(s, code, x, q, ss, syp, base, diss):
    ys, ts = [], []
    for layer in range(LAYERS):
        t = syp[layer] - (pick(code[layer], tables(False)[LOSS]) + ss[layer] if layer % 2 else ss[layer]) * x[layer]
        if layer % 2 == 0:
            t = t + diss[layer // 2] * pick(code[layer], tables(True)[INVERSE])
        ts.append(t)
        ys.append(q[layer] * t)
    return ys, ts


def begin(prev, diss, mat, cool, c_out, q_out, y0_out, m_out, s_ref, yp_ref):
    lane = lax.broadcasted_iota(jnp.int32, (8, TILE), 1)

    @pl.loop(0, CHUNKS)
    def _(k):
        rows = pl.ds(pl.multiple_of(8 * k, 8), 8)
        inner = pl.ds(pl.multiple_of(8 * k + 8, 8), 8)
        x = [field_rows(prev, diss, mat, cool, f, rows) for f in range(FIELDS)]
        for index, block in enumerate(strips_of(lambda f: x[f], lane)):
            c_out[index, rows, :] = block
        for layer in range(LAYERS):
            s = pick_inside(x[CODE + layer], tables(layer % 2 == 0)[ROOT])
            s_ref[layer, inner, :] = s
            for scen in range(SCEN):
                yp_ref[scen * LAYERS + layer, inner, :] = s * x[scen * LAYERS + layer]

    def body(k, acc):
        rows = pl.ds(pl.multiple_of(8 * k, 8), 8)
        r = pl.multiple_of(8 * k + 8, 8)
        s = rows_of(s_ref, 0, r)
        code = [field_rows(prev, diss, mat, cool, CODE + layer, rows) for layer in range(LAYERS)]
        ss = neighbours(s_ref, 0, r, s)
        q = []
        for layer in range(LAYERS):
            q.append(s[layer] / (pick_inside(code[layer], tables(layer % 2 == 0)[OVER]) + ss[layer]))
            q_out[layer, rows, :] = q[layer]
        sums = []
        for scen in range(SCEN):
            base = scen * LAYERS
            syp = neighbours(yp_ref, base, r, rows_of(yp_ref, base, r))
            x = [prev[scen, layer, rows] for layer in range(LAYERS)]
            d = [diss[scen, t, rows] for t in range(TIERS)]
            y, t = start_field(s, code, x, q, ss, syp, base, d)
            for layer in range(LAYERS):
                y0_out[base + layer, pl.ds(r, 8), :] = y[layer]
            sums.append(tree([a * b for a, b in zip(y, t)]))
        inside = (k > 0) & (k < CHUNKS - 1)
        return tuple(a + jnp.where(inside, b, 0.0) for a, b in zip(acc, sums))

    acc = lax.fori_loop(0, CHUNKS, body, (jnp.zeros((8, TILE), F32),) * SCEN)
    for scen in range(SCEN):
        m_out[scen] = acc[scen]


def messages(c_ref, a_in, b_in, a_out, b_out, halo_out, c_halo):
    lower = lax.axis_index("gx") % 2 == 0
    west = lax.axis_index("gy") % 2 == 0
    lane = lax.broadcasted_iota(jnp.int32, (8, TILE), 1)
    for field in range(FIELDS):
        rows = slice(HALO * field, HALO * (field + 1))
        a, b = a_in[rows, :], b_in[rows, :]
        halo_out[field, :HALO, :] = jnp.where(lower, b, a)
        halo_out[field, HALO:, :] = jnp.where(lower, a, b)
    slot = lane % GROUP // HALO
    odd = lane // GROUP % 2 == 1

    def send(blocks, rows):
        def arrange(base):
            p0, p1, code, d0, d1 = (turn(x, base + HALO * i) for x, i in zip(blocks, (0, 1, 2, 3, 3)))
            d = jnp.where(odd, turn(d1, GROUP), d0)
            return jnp.where(slot < 2, jnp.where(slot == 0, p0, p1), jnp.where(slot == 2, code, d))

        low, high = arrange(-8), arrange(-4)
        a_out[rows, :] = jnp.where(west, high, low)
        b_out[rows, :] = jnp.where(west, low, high)

    for k in range(CHUNKS):
        rows = slice(8 * k, 8 * k + 8)
        send([c_ref[i, rows, :] for i in range(5)], rows)
    blocks = strips_of(lambda f: halo_out[f], lane)
    for index in range(5):
        c_halo[index] = blocks[index]
    send(blocks, slice(TILE, TILE + 8))


def middle(prev, diss, mat, cool, halo, q_ref, y0, m_in, y1, y2, y0_fix, m_out, sn, ypn, y0n, y1n, y2n):
    zero = jnp.zeros((8, TILE), F32)

    def sweep(x_ref, out_ref):
        def body(k, acc):
            rows = pl.ds(pl.multiple_of(8 * k, 8), 8)
            r = pl.multiple_of(8 * k + 8, 8)
            odd, even = [], []
            for scen in range(SCEN):
                base = scen * LAYERS
                x = rows_of(x_ref, base, r)
                t = neighbours(x_ref, base, r, x)
                odd.append(tree([a * b for a, b in zip(x, t)]))
                if out_ref is not None:
                    p = []
                    for layer in range(LAYERS):
                        y = q_ref[layer, rows, :] * t[layer]
                        out_ref[base + layer, pl.ds(r, 8), :] = y
                        p.append(y * t[layer])
                    even.append(tree(p))
            inside = (k > 0) & (k < CHUNKS - 1)
            return tuple(a + jnp.where(inside, b, 0.0) for a, b in zip(acc, odd + even))

        return lax.fori_loop(0, CHUNKS, body, (zero,) * (SCEN if out_ref is None else 2 * SCEN))

    m = [m_in[scen] for scen in range(SCEN)]
    m += sweep(y0, y1)
    m += sweep(y1, y2)
    m += sweep(y2, None)

    for side in range(2):
        own = 16 if side == 0 else 8
        beyond = 24 - own
        near = slice(0, 8) if side == 0 else slice(TILE - 8, TILE)
        inner = slice(8, 16) if side == 0 else slice(TILE - 16, TILE - 8)
        inner_at = 24 if side == 0 else 0
        chunks = (
            (own, lambda f: field_rows(prev, diss, mat, cool, f, near)),
            (inner_at, lambda f: field_rows(prev, diss, mat, cool, f, inner)),
            (beyond, lambda f: turn(halo[f], 4, 0)),
        )
        for at, get in chunks:
            for layer in range(LAYERS):
                s = pick(get(CODE + layer), tables(layer % 2 == 0)[ROOT])
                sn[layer, at : at + 8, :] = s
                for scen in range(SCEN):
                    ypn[scen * LAYERS + layer, at : at + 8, :] = s * get(scen * LAYERS + layer)
        padded_inner = slice(inner.start + 8, inner.stop + 8)
        padded_near = slice(near.start + 8, near.stop + 8)
        fix = slice(8 * side, 8 * side + 8)
        for f in range(PAIRS):
            y0n[f, inner_at : inner_at + 8, :] = y0[f, padded_inner, :]
            y1n[f, inner_at : inner_at + 8, :] = y1[f, padded_inner, :]
            y2n[f, inner_at : inner_at + 8, :] = y2[f, padded_inner, :]
        q = {}
        for at, get in (chunks[0], chunks[2]):
            s = rows_of(sn, 0, at)
            ss = neighbours(sn, 0, at, s)
            code = [get(CODE + layer) for layer in range(LAYERS)]
            q[at] = [s[i] / (pick(code[i], tables(i % 2 == 0)[OVER]) + ss[i]) for i in range(LAYERS)]
            for scen in range(SCEN):
                base = scen * LAYERS
                syp = neighbours(ypn, base, at, rows_of(ypn, base, at))
                x = [get(base + layer) for layer in range(LAYERS)]
                d = [get(DISS + scen * TIERS + t) for t in range(TIERS)]
                y, t = start_field(s, code, x, q[at], ss, syp, base, d)
                for layer in range(LAYERS):
                    y0n[base + layer, at : at + 8, :] = y[layer]
                    if at == own:
                        y0_fix[base + layer, fix, :] = y[layer]
                if at == own:
                    m[scen] = m[scen] + tree([a * b for a, b in zip(y, t)])
        for level, (x_ref, n_ref, out_ref) in enumerate(((y0n, y1n, y1), (y1n, y2n, y2), (y2n, None, None))):
            for at in (own, beyond) if n_ref is not None else (own,):
                for scen in range(SCEN):
                    base = scen * LAYERS
                    x = rows_of(x_ref, base, at)
                    t = neighbours(x_ref, base, at, x)
                    if at == own:
                        index = SCEN * (2 * level + 1) + scen
                        m[index] = m[index] + tree([a * b for a, b in zip(x, t)])
                    if n_ref is None:
                        continue
                    p = []
                    for layer in range(LAYERS):
                        y = q[at][layer] * t[layer]
                        n_ref[base + layer, at : at + 8, :] = y
                        if at == own:
                            out_ref[base + layer, padded_near, :] = y
                            p.append(y * t[layer])
                    if at == own:
                        index = SCEN * (2 * level + 2) + scen
                        m[index] = m[index] + tree(p)
    for index in range(SCEN * MOMENTS):
        m_out[index] = m[index]


TOP = 16
ROWS = TOP + TILE + 16


def strips(c_ref, c_halo, a_in, b_in, m_in, ys_out, m_out, code_ref, s_ref, x_ref, d_ref, yp_ref, q_ref, y0, y1, y2):
    west = lax.axis_index("gy") % 2 == 0
    lane = lax.broadcasted_iota(jnp.int32, (8, TILE), 1)
    place = lane % GROUP
    real = lane < GROUP * LAYERS
    tier = lane // GROUP % 2 == 0
    zero = jnp.zeros((8, TILE), F32)
    sides = (
        (place < 8, (place >= 8) & (place < 12) & real, (place >= 4) & (place < 8) & real, 8),
        (place >= 8, (place >= 4) & (place < 8) & real, (place >= 8) & (place < 12) & real, 4),
    )

    def lookup(code, kind):
        out = zero if tables(True)[kind][0] == 0.0 else jnp.full_like(zero, tables(True)[kind][0])
        for index in range(1, 5):
            value = jnp.where(tier, F32(tables(True)[kind][index]), F32(tables(False)[kind][index]))
            out = jnp.where(code == float(index), value, out)
        return out

    chunk_rows = [(slice(8 * k, 8 * k + 8), (8 * k + TOP,), 0) for k in range(CHUNKS)]
    chunk_rows.append((None, (TOP - 8, TOP + TILE), 4))
    for rows, targets, rotation in chunk_rows:
        message = slice(TILE, TILE + 8) if rows is None else rows
        a, b = a_in[message, :], b_in[message, :]
        blocks = [c_halo[i] if rows is None else c_ref[i, rows, :] for i in range(5)]
        for side, (own, beyond, _, base) in enumerate(sides):
            got = jnp.where(west, a, b) if side == 0 else jnp.where(west, b, a)
            full = []
            for index, shift in enumerate((base, base - 4, base - 8, base - 12, base - 12 - GROUP)):
                mask = beyond if index < 3 else beyond & tier
                full.append(jnp.where(own, blocks[index], jnp.where(mask, turn(got, shift), zero)))
            full = [turn(x, rotation, 0) for x in full]
            s = lookup(full[2], ROOT)
            for at in targets:
                here = slice(at, at + 8)
                code_ref[side, here, :] = full[2]
                s_ref[side, here, :] = s
                for scen in range(SCEN):
                    x_ref[2 * scen + side, here, :] = full[scen]
                    d_ref[2 * scen + side, here, :] = full[3 + scen]
                    yp_ref[2 * scen + side, here, :] = s * full[scen]

    def around(ref, index, at):
        x = ref[index, at : at + 8, :]
        lateral = (ref[index, at - 1 : at + 7, :] + ref[index, at + 1 : at + 9, :]) + (turn(x, 1) + turn(x, -1))
        return x, lateral + VERTICAL * (turn(x, GROUP) + turn(x, -GROUP))

    everywhere = range(TOP - 8, TOP + TILE + 8, 8)
    within = range(TOP, TOP + TILE, 8)
    m = [[zero, zero] for _ in range(SCEN * MOMENTS)]

    def count(index, side, at, value):
        if at in within:
            m[index][side] = m[index][side] + value

    for at in everywhere:
        here = slice(at, at + 8)
        for side in range(2):
            code = code_ref[side, here, :]
            s, ss = around(s_ref, side, at)
            q = s / (lookup(code, OVER) + ss)
            q_ref[side, here, :] = q
            inverse, loss = lookup(code, INVERSE), lookup(code, LOSS) + ss
            for scen in range(SCEN):
                f = 2 * scen + side
                _, syp = around(yp_ref, f, at)
                t = syp - loss * x_ref[f, here, :] + d_ref[f, here, :] * inverse
                y = q * t
                y0[f, here, :] = y
                count(scen, side, at, y * t)
    for level, (ref, out) in enumerate(((y0, y1), (y1, y2), (y2, None))):
        for at in everywhere if out is not None else within:
            here = slice(at, at + 8)
            for side in range(2):
                for scen in range(SCEN):
                    f = 2 * scen + side
                    x, t = around(ref, f, at)
                    count(SCEN * (2 * level + 1) + scen, side, at, x * t)
                    if out is not None:
                        y = q_ref[side, here, :] * t
                        out[f, here, :] = y
                        count(SCEN * (2 * level + 2) + scen, side, at, y * t)
    for level, ref in enumerate((y0, y1, y2)):
        for scen in range(SCEN):
            for k in range(CHUNKS):
                here = slice(8 * k + TOP, 8 * k + TOP + 8)
                merged = jnp.where(place < 8, ref[2 * scen, here, :], ref[2 * scen + 1, here, :])
                ys_out[SCEN * level + scen, 8 * k : 8 * k + 8, :] = merged
    line = lax.broadcasted_iota(jnp.int32, (8, TILE), 1)
    inner = (lane >= HALO) & (lane < TILE - HALO)
    out = zero
    for index in range(SCEN * MOMENTS):
        east, wst = (jnp.where(sides[side][2], m[index][side], 0.0) for side in range(2))
        value = jnp.where(inner, m_in[index], 0.0) + (east + wst)
        value = jnp.sum(jnp.sum(value, axis=0, keepdims=True), axis=1, keepdims=True)
        out = jnp.where(line == index, value, out)
    m_out[...] = jnp.broadcast_to(out, m_out.shape)


def combine(prev, mat, cool, y0, y0_fix, y1, y2, ys, m_ref, out, buffer, sems):
    lane = lax.broadcasted_iota(jnp.int32, (8, TILE), 1)
    edge = (lane < HALO) | (lane >= TILE - HALO)
    total = tree([m_ref[i] for i in range(m_ref.shape[0])])
    total = jnp.broadcast_to(jnp.sum(total, axis=0, keepdims=True), (8, TILE))
    weights = coefficients([turn(total, -SCEN * i) for i in range(MOMENTS)])
    c = [
        [jnp.broadcast_to(jnp.sum(jnp.where(lane == scen, w, 0.0), axis=1, keepdims=True), (8, TILE)) for w in weights]
        for scen in range(SCEN)
    ]
    parts = 4
    copies = []

    def chunk(k, at, first):
        rows = pl.ds(at, 8)
        padded = pl.ds(at + 8, 8)
        scale = [
            pick_inside(field_rows(prev, None, mat, cool, CODE + layer, rows), tables(layer % 2 == 0)[INVERSE])
            for layer in range(LAYERS)
        ]
        for scen in range(SCEN):
            strip = tree([c[scen][i] * ys[SCEN * i + scen, rows, :] for i in range(3)])
            for layer in range(LAYERS):
                f = scen * LAYERS + layer
                value = c[scen][1] * y1[f, padded, :] + c[scen][2] * y2[f, padded, :] + c[scen][0] * first(f)
                value = jnp.where(edge, turn(strip, 120 - GROUP * layer), value)
                buffer[scen, layer, rows, :] = prev[scen, layer, rows] + scale[layer] * value

    for part in range(parts):
        if part == 0:
            chunk(0, 0, lambda f: y0_fix[f, 0:8, :])
        low = max(1, part * CHUNKS // parts)
        high = min(CHUNKS - 1, (part + 1) * CHUNKS // parts)

        @pl.loop(low, high)
        def _(k):
            at = pl.multiple_of(8 * k, 8)
            chunk(k, at, lambda f: y0[f, pl.ds(at + 8, 8), :])

        if part == parts - 1:
            chunk(CHUNKS - 1, TILE - 8, lambda f: y0_fix[f, 8:16, :])
        rows = pl.ds(part * TILE // parts, TILE // parts)
        copy = pltpu.make_async_copy(buffer.at[:, :, rows], out.at[:, :, rows], sems.at[part])
        copy.start()
        copies.append(copy)
    for copy in copies:
        copy.wait()


def swaps(devices):
    near = [(i, i ^ 1) for i in range(devices)]
    far = [(i, i + 1) for i in range(1, devices - 1, 2)]
    return near, far + [(b, a) for a, b in far]


def exchange(a, b, axis):
    near, far = swaps(lax.axis_size(axis))
    return lax.ppermute(a, axis, near), lax.ppermute(b, axis, far)


def coefficients(m):
    h11, h12, h13, h23, h33 = (m[i] - m[i + 1] for i in range(5))
    h22 = h13

    def inverse(x):
        return jnp.where(x > 0, 1.0 / jnp.where(x > 0, x, 1.0), 0.0)

    d1 = inverse(h11)
    l21, l31 = h12 * d1, h13 * d1
    d2 = inverse(h22 - l21 * h12)
    u23 = h23 - l31 * h12
    l32 = u23 * d2
    d3 = inverse(h33 - l31 * h13 - l32 * u23)
    g1 = m[0]
    g2 = m[1] - l21 * g1
    g3 = m[2] - l31 * g1 - l32 * g2
    c3 = g3 * d3
    c2 = g2 * d2 - l32 * c3
    c1 = g1 * d1 - l21 * c2 - l31 * c3
    return c1, c2, c3


def vmem(n):
    return [pl.BlockSpec(memory_space=pltpu.VMEM)] * n


def shape(*dims):
    return jax.ShapeDtypeStruct(dims, F32)


def call(kernel, inputs, outputs, scratch, mib, flops, in_specs=None, out_specs=None):
    many = isinstance(outputs, list)
    return pl.pallas_call(
        kernel,
        in_specs=in_specs or vmem(len(inputs)),
        out_specs=out_specs or (vmem(len(outputs)) if many else vmem(1)[0]),
        out_shape=outputs,
        scratch_shapes=scratch,
        compiler_params=pltpu.CompilerParams(vmem_limit_bytes=int(mib * 2**20)),
        cost_estimate=pl.CostEstimate(flops=flops, bytes_accessed=1 << 20, transcendentals=0),
    )(*inputs)


def per_device(previous, dissipated, material, coolant):
    given = (previous, dissipated, material, coolant)

    def buffer(dtype, *dims):
        return pltpu.VMEM(dims, dtype)

    edges = []
    for a in given:
        edges += [buffer(a.dtype, *a.shape[:-2], 8, TILE)] * 2
    a, b = call(
        pack_rows,
        given,
        [shape(FIELDS * HALO, TILE)] * 2,
        edges + [pltpu.SemaphoreType.DMA((8,))],
        62,
        1 << 20,
        in_specs=[pl.BlockSpec(memory_space=pltpu.HBM)] * 4,
    )
    a, b = exchange(a, b, "gx")
    padded = TILE + 16
    c_blocks, q, y0, m0 = call(
        begin,
        given,
        [shape(5, TILE, TILE), shape(LAYERS, TILE, TILE), shape(PAIRS, padded, TILE), shape(SCEN, 8, TILE)],
        [buffer(F32, LAYERS, padded, TILE), buffer(F32, PAIRS, padded, TILE)],
        8,
        1 << 27,
    )
    a, b, halo, c_halo = call(
        messages,
        (c_blocks, a, b),
        [shape(TILE + 8, TILE)] * 2 + [shape(FIELDS, 8, TILE), shape(5, 8, TILE)],
        [],
        4,
        1 << 20,
    )
    a, b = exchange(a, b, "gy")
    y1, y2, y0_fix, m = call(
        middle,
        (*given, halo, q, y0, m0),
        [shape(PAIRS, padded, TILE)] * 2 + [shape(PAIRS, 16, TILE), shape(SCEN * MOMENTS, 8, TILE)],
        [buffer(F32, LAYERS, 32, TILE)] + [buffer(F32, PAIRS, 32, TILE)] * 4,
        8,
        1 << 27,
    )
    devices = lax.axis_size("gx") * lax.axis_size("gy")
    ys, m = call(
        strips,
        (c_blocks, c_halo, a, b, m),
        [shape(3 * SCEN, TILE, TILE), shape(devices // 8, 8, TILE)],
        [buffer(F32, n, ROWS, TILE) for n in (2, 2, 4, 4, 4, 2, 4, 4, 4)],
        8,
        1 << 24,
    )
    everything = lax.all_to_all(m.reshape(devices, 1, TILE), ("gx", "gy"), split_axis=0, concat_axis=0, tiled=True)
    return call(
        combine,
        (previous, material, coolant, y0, y0_fix, y1, y2, ys, everything.reshape(devices // 8, 8, TILE)),
        shape(*previous.shape),
        [buffer(F32, *previous.shape), pltpu.SemaphoreType.DMA((4,))],
        8,
        1 << 24,
        out_specs=pl.BlockSpec(memory_space=pltpu.HBM),
    )


def solution(mesh):
    placed = (P(None, None, "gx", "gy"),) * 2 + (P(None, "gx", "gy"),) * 2
    return jax.shard_map(
        per_device, mesh=mesh, in_specs=placed, out_specs=P(None, None, "gx", "gy"), check_vma=False
    )
```

time: 231 us -> 51.7 us (0.22)
  blocking collectives: 85.6 us -> 27.7 us
  local copies, waits for them, and re-layouts: 52.2 us -> 0.02 us
  starting transfers between devices: 53.5 us -> 6.96 us
  other arithmetic: 37.2 us -> 0 us
  Pallas kernels: 0 us -> 16.6 us
    all_to_all x6 -> x1, blocking collectives: 85.6 us -> 27.7 us  [per_device(): lax.all_to_all(m.reshape(devices, 1, TILE), ('gx', 'gy'), split_axis=0, c...]
    ppermute x20 -> x4, starting transfers between devices: 53.5 us -> 6.96 us  [exchange(): return (lax.ppermute(a, axis, near), lax.ppermute(b, axis, far))]
    slice x17 -> x0, local copies, waits for them, and re-layouts: 18.7 us -> none  [the longest x10 10.9 us: extended_2(): last = lax.slice_in_dim(x, length - width, length, axis=dim)]
    pallas_call x0 -> x6, Pallas kernels: none -> 16.6 us  [call(): pl.pallas_call(kernel, in_specs=in_specs or vmem(len(inputs)), out_specs=...]
    reduce_sum x10 -> x0, other arithmetic: 16.1 us -> none  [the longest x4 15.9 us: core_sum(): return jnp.sum(first * second, axis=(1, 2, 3))]
    unnamed x44 -> x8, local copies, waits for them, and re-layouts: 13.3 us -> 0.02 us
    ppermute x6 -> x0, local copies, waits for them, and re-layouts: 8.17 us -> none  [the longest x3 4.09 us: extended_2(): lax.ppermute(last, axis, up)]
    div x6 -> x0, other arithmetic: 7.6 us -> none  [the longest x3 7.37 us: per_device(): scaled = residual / diagonal]
  transfers between devices with their start and end apart: 20 -> 4, of which waited for: 0 -> 1; matrix products, arithmetic and copies ran while one was open for 23% -> 0% of each run, Pallas kernels for 0% -> 19%
where the time goes in v2:
time: 51.7 us; the launch traced here: 51.5 us
  blocking collectives  27.7 us (54%)
  Pallas kernels  16.6 us (32%)
  starting transfers between devices  6.96 us (13%)
    all_to_all x1, blocking collectives, per_device(): lax.all_to_all(m.reshape(devices, 1, TILE), ('gx', 'gy'), split_axis=0, c...  27.7 us
    pallas_call x6, Pallas kernels, call(): pl.pallas_call(kernel, in_specs=in_specs or vmem(len(inputs)), out_specs=...  16.6 us
    ppermute x4, starting transfers between devices, exchange(): return (lax.ppermute(a, axis, near), lax.ppermute(b, axis, far))  6.96 us
  transfers between devices with their start and end apart: 4, of which 1 were waited for; matrix products, arithmetic and copies ran while one was open for 0% of the time, Pallas kernels for 19%

profile of v2, /device:TPU:1, one launch (start us, length us, event | category | flops | bytes accessed | tf_op | source)
XLA Modules:
  0.0 51.5 jit_solution(7979764099585026968)
XLA Ops:
  0.0 0.0 copy-start.3
  0.0 0.0 copy-start.2
  0.0 0.0 copy-start
  0.0 0.0 copy-start.1
  0.0 1.7 %shard_map.47 = (f32[116,128]{1,0:T(8,128)}, f32[116,128]{1,0:T(8,128)}) custom-call(f32[2,7,128,128]{3,2,1,0:T(8,128)} %prev.7, f32[2,4,128,128]{3,2,1,0:T(8,128)} %diss.5, s32[4,128,128]{2,1,0:T(8,128)} %mat.7, s32[3,128,128]{2,1,0:T(8,128)} %cool.7), custom_call_target="tpu_custom_call" | custom-call | flops 1048576 | bytes 1048576 | tf_op jit(solution)/shard_map/pallas_call | solution.py:515
  1.8 3.3 %collective-permute-start = (f32[116,128]{1,0:T(8,128)}, f32[116,128]{1,0:T(8,128)S(1)}, u32[]{:S(2)}, u32[]{:S(2)}) collective-permute-start(f32[116,128]{1,0:T(8,128)} %get-tuple-element.23), channel_id=1, source_target_pairs={{0,32},{32,0},{64,96},{96,64},{128,160},{160,128},{192,224},{224,1... | collective-permute-start | bytes 178184 | tf_op jit(solution)/shard_map/ppermute | solution.py:480
  5.0 1.9 %collective-permute-start.1 = (f32[116,128]{1,0:T(8,128)}, f32[116,128]{1,0:T(8,128)S(1)}, u32[]{:S(2)}, u32[]{:S(2)}) collective-permute-start(f32[116,128]{1,0:T(8,128)} %get-tuple-element.24), channel_id=1, source_target_pairs={{32,64},{96,128},{160,192},{64,32},{128,96},{192,160},{33,65},{97,... | collective-permute-start | bytes 178184 | tf_op jit(solution)/shard_map/ppermute | solution.py:480
  7.0 0.0 copy-done.3
  7.0 0.0 copy-done.2
  7.0 0.0 copy-done
  7.0 0.0 copy-done.1
  7.0 3.7 %shard_map.46 = (f32[5,128,128]{2,1,0:T(8,128)S(1)}, f32[7,128,128]{2,1,0:T(8,128)S(1)}, f32[14,144,128]{2,1,0:T(8,128)S(1)}, f32[2,8,128]{2,1,0:T(8,128)S(1)}) custom-call(f32[2,7,128,128]{3,2,1,0:T(8,128)S(1)} %copy-done, f32[2,4,128,128]{3,2,1,0:T(8,128)S(1)} %copy-done.1, s32[4,128,128]{2,1,0:T(8,128)S(1)} %copy-done.2, s32[3,128,128]{2,1,0:T(8,128)S(1)} %copy-done.3), custom_call_target="tpu_custom_call" | custom-call | flops 134217728 | bytes 1048576 | tf_op jit(solution)/shard_map/pallas_call | solution.py:515
  10.7 0.0 collective-permute-done.a_in
  10.7 0.1 collective-permute-done.1.b_in
  10.8 1.2 %shard_map.48 = (f32[136,128]{1,0:T(8,128)S(1)}, f32[136,128]{1,0:T(8,128)S(1)}, f32[29,8,128]{2,1,0:T(8,128)S(1)}, f32[5,8,128]{2,1,0:T(8,128)S(1)}) custom-call(f32[5,128,128]{2,1,0:T(8,128)S(1)} %get-tuple-element.22.c_ref, f32[116,128]{1,0:T(8,128)S(1)} %collective-permute-done.a_in, f32[116,128]{1,0:T(8,128)S(1)} %collective-permute-done.1.b_in), custom_call_target="tpu_custom_call" | custom-call | flops 1048576 | bytes 1048576 | tf_op jit(solution)/shard_map/pallas_call | solution.py:515
  12.0 1.1 %collective-permute-start.2 = (f32[136,128]{1,0:T(8,128)S(1)}, f32[136,128]{1,0:T(8,128)S(1)}, u32[]{:S(2)}, u32[]{:S(2)}) collective-permute-start(f32[136,128]{1,0:T(8,128)S(1)} %get-tuple-element.32), channel_id=1, source_target_pairs={{0,1},{1,0},{2,3},{3,2},{4,5},{5,4},{6,7},{7,6},{8,9},{9,8},{10,11... | collective-permute-start | bytes 208904 | tf_op jit(solution)/shard_map/ppermute | solution.py:480
  13.1 0.7 %collective-permute-start.3 = (f32[136,128]{1,0:T(8,128)S(1)}, f32[136,128]{1,0:T(8,128)S(1)}, u32[]{:S(2)}, u32[]{:S(2)}) collective-permute-start(f32[136,128]{1,0:T(8,128)S(1)} %get-tuple-element.33), channel_id=1, source_target_pairs={{1,2},{3,4},{5,6},{7,8},{9,10},{11,12},{13,14},{15,16},{17,18},{19... | collective-permute-start | bytes 208904 | tf_op jit(solution)/shard_map/ppermute | solution.py:480
  13.8 6.0 %shard_map.49 = (f32[14,144,128]{2,1,0:T(8,128)S(1)}, f32[14,144,128]{2,1,0:T(8,128)S(1)}, f32[14,16,128]{2,1,0:T(8,128)S(1)}, f32[12,8,128]{2,1,0:T(8,128)S(1)}) custom-call(f32[2,7,128,128]{3,2,1,0:T(8,128)S(1)} %copy-done, f32[2,4,128,128]{3,2,1,0:T(8,128)S(1)} %copy-done.1, s32[4,128,128]{2,1,0:T(8,128)S(1)} %copy-done.2, s32[3,128,128]{2,1,0:T(8,128)S(1)} %copy-done.3, ...), custom_call_target="tpu_custom_call" | custom-call | flops 134217728 | bytes 1048576 | tf_op jit(solution)/shard_map/pallas_call | solution.py:515
  19.7 0.0 collective-permute-done.2.a_in
  19.8 0.0 collective-permute-done.3.b_in
  19.8 1.7 %shard_map.50 = (f32[6,128,128]{2,1,0:T(8,128)S(1)}, f32[32,8,128]{2,1,0:T(8,128)S(1)}) custom-call(f32[5,128,128]{2,1,0:T(8,128)S(1)} %get-tuple-element.22.c_ref, f32[5,8,128]{2,1,0:T(8,128)S(1)} %get-tuple-element.31.c_halo, f32[136,128]{1,0:T(8,128)S(1)} %collective-permute-done.2.a_in, f32[136,128]{1,0:T(8,128)S(1)} %collective-permute-done.3.b_in, ...), custom_call_target="tpu_custom_call" | custom-call | flops 16777216 | bytes 1048576 | tf_op jit(solution)/shard_map/pallas_call | solution.py:515
  21.5 27.7 %all_to_all.5 = f32[256,1,128]{2,1,0:T(1,128)S(1)} all-to-all(f32[256,1,128]{2,1,0:T(1,128)S(1)} %bitcast.5), channel_id=1, replica_groups=mesh['gx'=8,'gy'=32] {'gx','gy'}, dimensions={0} | all-to-all | bytes 262144 | tf_op jit(solution)/shard_map/all_to_all | solution.py:580
  49.2 2.4 %shard_map.51 = f32[2,7,128,128]{3,2,1,0:T(8,128)} custom-call(f32[2,7,128,128]{3,2,1,0:T(8,128)S(1)} %copy-done, s32[4,128,128]{2,1,0:T(8,128)S(1)} %copy-done.2, s32[3,128,128]{2,1,0:T(8,128)S(1)} %copy-done.3, f32[14,144,128]{2,1,0:T(8,128)S(1)} %get-tuple-element.21.y0, f32[14,16,128]{2,1,0:T(8,128)S(1)} %get-tuple-element.28.y0_fix, ...), custom_call_target="tpu_custom_call" | custom-call | flops 16777216 | bytes 1048576 | tf_op jit(solution)/shard_map/pallas_call | solution.py:515
Async XLA Ops:
  0.0 7.0 %copy-start.3 = (s32[3,128,128]{2,1,0:T(8,128)S(1)}, s32[3,128,128]{2,1,0:T(8,128)}, u32[]{:S(2)}) copy-start(s32[3,128,128]{2,1,0:T(8,128)} %cool.7) | copy-start | bytes 589828
  0.0 7.0 %copy-start.2 = (s32[4,128,128]{2,1,0:T(8,128)S(1)}, s32[4,128,128]{2,1,0:T(8,128)}, u32[]{:S(2)}) copy-start(s32[4,128,128]{2,1,0:T(8,128)} %mat.7) | copy-start | bytes 786436
  0.0 7.0 %copy-start = (f32[2,7,128,128]{3,2,1,0:T(8,128)S(1)}, f32[2,7,128,128]{3,2,1,0:T(8,128)}, u32[]{:S(2)}) copy-start(f32[2,7,128,128]{3,2,1,0:T(8,128)} %prev.7) | copy-start | bytes 2752516
  0.0 7.0 %copy-start.1 = (f32[2,4,128,128]{3,2,1,0:T(8,128)S(1)}, f32[2,4,128,128]{3,2,1,0:T(8,128)}, u32[]{:S(2)}) copy-start(f32[2,4,128,128]{3,2,1,0:T(8,128)} %diss.5) | copy-start | bytes 1572868
  1.8 8.9 %collective-permute-start = (f32[116,128]{1,0:T(8,128)}, f32[116,128]{1,0:T(8,128)S(1)}, u32[]{:S(2)}, u32[]{:S(2)}) collective-permute-start(f32[116,128]{1,0:T(8,128)} %get-tuple-element.23), channel_id=1, source_target_pairs={{0,32},{32,0},{64,96},{96,64},{128,160},{160,128},{192,224},{224,1... | collective-permute-start | bytes 178184 | tf_op jit(solution)/shard_map/ppermute | solution.py:480
  5.0 5.7 %collective-permute-start.1 = (f32[116,128]{1,0:T(8,128)}, f32[116,128]{1,0:T(8,128)S(1)}, u32[]{:S(2)}, u32[]{:S(2)}) collective-permute-start(f32[116,128]{1,0:T(8,128)} %get-tuple-element.24), channel_id=1, source_target_pairs={{32,64},{96,128},{160,192},{64,32},{128,96},{192,160},{33,65},{97,... | collective-permute-start | bytes 178184 | tf_op jit(solution)/shard_map/ppermute | solution.py:480
  12.0 7.8 %collective-permute-start.2 = (f32[136,128]{1,0:T(8,128)S(1)}, f32[136,128]{1,0:T(8,128)S(1)}, u32[]{:S(2)}, u32[]{:S(2)}) collective-permute-start(f32[136,128]{1,0:T(8,128)S(1)} %get-tuple-element.32), channel_id=1, source_target_pairs={{0,1},{1,0},{2,3},{3,2},{4,5},{5,4},{6,7},{7,6},{8,9},{9,8},{10,11... | collective-permute-start | bytes 208904 | tf_op jit(solution)/shard_map/ppermute | solution.py:480
  13.1 6.7 %collective-permute-start.3 = (f32[136,128]{1,0:T(8,128)S(1)}, f32[136,128]{1,0:T(8,128)S(1)}, u32[]{:S(2)}, u32[]{:S(2)}) collective-permute-start(f32[136,128]{1,0:T(8,128)S(1)} %get-tuple-element.33), channel_id=1, source_target_pairs={{1,2},{3,4},{5,6},{7,8},{9,10},{11,12},{13,14},{15,16},{17,18},{19... | collective-permute-start | bytes 208904 | tf_op jit(solution)/shard_map/ppermute | solution.py:480

commit v3 on v2

--- a/solution.py
+++ b/solution.py
@@ -148,10 +148,9 @@
 def begin(prev, diss, mat, cool, c_out, q_out, y0_out, m_out, s_ref, yp_ref):
     lane = lax.broadcasted_iota(jnp.int32, (8, TILE), 1)
 
-    @pl.loop(0, CHUNKS)
-    def _(k):
-        rows = pl.ds(pl.multiple_of(8 * k, 8), 8)
-        inner = pl.ds(pl.multiple_of(8 * k + 8, 8), 8)
+    for k in range(CHUNKS):
+        rows = slice(8 * k, 8 * k + 8)
+        inner = slice(8 * k + 8, 8 * k + 16)
         x = [field_rows(prev, diss, mat, cool, f, rows) for f in range(FIELDS)]
         for index, block in enumerate(strips_of(lambda f: x[f], lane)):
             c_out[index, rows, :] = block
@@ -161,9 +160,10 @@
             for scen in range(SCEN):
                 yp_ref[scen * LAYERS + layer, inner, :] = s * x[scen * LAYERS + layer]
 
-    def body(k, acc):
-        rows = pl.ds(pl.multiple_of(8 * k, 8), 8)
-        r = pl.multiple_of(8 * k + 8, 8)
+    acc = [jnp.zeros((8, TILE), F32)] * SCEN
+    for k in range(CHUNKS):
+        rows = slice(8 * k, 8 * k + 8)
+        r = 8 * k + 8
         s = rows_of(s_ref, 0, r)
         code = [field_rows(prev, diss, mat, cool, CODE + layer, rows) for layer in range(LAYERS)]
         ss = neighbours(s_ref, 0, r, s)
@@ -181,10 +181,8 @@
             for layer in range(LAYERS):
                 y0_out[base + layer, pl.ds(r, 8), :] = y[layer]
             sums.append(tree([a * b for a, b in zip(y, t)]))
-        inside = (k > 0) & (k < CHUNKS - 1)
-        return tuple(a + jnp.where(inside, b, 0.0) for a, b in zip(acc, sums))
-
-    acc = lax.fori_loop(0, CHUNKS, body, (jnp.zeros((8, TILE), F32),) * SCEN)
+        if 0 < k < CHUNKS - 1:
+            acc = [a + b for a, b in zip(acc, sums)]
     for scen in range(SCEN):
         m_out[scen] = acc[scen]
 
@@ -224,9 +222,12 @@
     zero = jnp.zeros((8, TILE), F32)
 
     def sweep(x_ref, out_ref):
-        def body(k, acc):
-            rows = pl.ds(pl.multiple_of(8 * k, 8), 8)
-            r = pl.multiple_of(8 * k + 8, 8)
+        acc = [zero] * (SCEN if out_ref is None else 2 * SCEN)
+        for k in range(CHUNKS):
+            if out_ref is None and k in (0, CHUNKS - 1):
+                continue
+            rows = slice(8 * k, 8 * k + 8)
+            r = 8 * k + 8
             odd, even = [], []
             for scen in range(SCEN):
                 base = scen * LAYERS
@@ -240,10 +241,9 @@
                         out_ref[base + layer, pl.ds(r, 8), :] = y
                         p.append(y * t[layer])
                     even.append(tree(p))
-            inside = (k > 0) & (k < CHUNKS - 1)
-            return tuple(a + jnp.where(inside, b, 0.0) for a, b in zip(acc, odd + even))
-
-        return lax.fori_loop(0, CHUNKS, body, (zero,) * (SCEN if out_ref is None else 2 * SCEN))
+            if 0 < k < CHUNKS - 1:
+                acc = [a + b for a, b in zip(acc, odd + even)]
+        return acc
 
     m = [m_in[scen] for scen in range(SCEN)]
     m += sweep(y0, y1)
@@ -454,10 +454,8 @@
         low = max(1, part * CHUNKS // parts)
         high = min(CHUNKS - 1, (part + 1) * CHUNKS // parts)
 
-        @pl.loop(low, high)
-        def _(k):
-            at = pl.multiple_of(8 * k, 8)
-            chunk(k, at, lambda f: y0[f, pl.ds(at + 8, 8), :])
+        for k in range(low, high):
+            chunk(k, 8 * k, lambda f, at=8 * k: y0[f, pl.ds(at + 8, 8), :])
 
         if part == parts - 1:
             chunk(CHUNKS - 1, TILE - 8, lambda f: y0_fix[f, 8:16, :])
@@ -542,11 +540,11 @@
         in_specs=[pl.BlockSpec(memory_space=pltpu.HBM)] * 4,
     )
     a, b = exchange(a, b, "gx")
-    padded = TILE + 16
+    padded = TILE + 24
     c_blocks, q, y0, m0 = call(
         begin,
         given,
-        [shape(5, TILE, TILE), shape(LAYERS, TILE, TILE), shape(PAIRS, padded, TILE), shape(SCEN, 8, TILE)],
+        [shape(5, TILE, TILE), shape(LAYERS, TILE + 8, TILE), shape(PAIRS, padded, TILE), shape(SCEN, 8, TILE)],
         [buffer(F32, LAYERS, padded, TILE), buffer(F32, PAIRS, padded, TILE)],
         8,
         1 << 27,

time: 51.7 us -> 49.1 us (0.950)
  Pallas kernels: 16.6 us -> 9.47 us
  blocking collectives: 27.7 us -> 30.6 us
  waiting for transfers between devices: 0.12 us -> 2.75 us
  starting transfers between devices: 6.96 us -> 5.94 us
    pallas_call x6, Pallas kernels: 16.6 us -> 9.47 us  [call(): pl.pallas_call(kernel, in_specs=in_specs or vmem(len(inputs)), out_specs=...]
    all_to_all x1, blocking collectives: 27.7 us -> 30.6 us  [per_device(): lax.all_to_all(m.reshape(devices, 1, TILE), ('gx', 'gy'), split_axis=0, c...]
    ppermute x4, waiting for transfers between devices: 0.12 us -> 2.75 us  [exchange(): return (lax.ppermute(a, axis, near), lax.ppermute(b, axis, far))]
    ppermute x4, starting transfers between devices: 6.96 us -> 5.94 us  [exchange(): return (lax.ppermute(a, axis, near), lax.ppermute(b, axis, far))]
  transfers between devices with their start and end apart: 4 -> 4, of which waited for: 1 -> 2; matrix products, arithmetic and copies ran while one was open for 0% -> 0% of each run, Pallas kernels for 19% -> 7%
where the time goes in v3:
time: 49.1 us; the launch traced here: 48.9 us
  blocking collectives  30.6 us (62%)
  Pallas kernels  9.47 us (19%)
  starting transfers between devices  5.94 us (12%)
  waiting for transfers between devices  2.75 us (6%)
    all_to_all x1, blocking collectives, per_device(): lax.all_to_all(m.reshape(devices, 1, TILE), ('gx', 'gy'), split_axis=0, c...  30.6 us
    pallas_call x6, Pallas kernels, call(): pl.pallas_call(kernel, in_specs=in_specs or vmem(len(inputs)), out_specs=...  9.47 us
    ppermute x4, starting transfers between devices, exchange(): return (lax.ppermute(a, axis, near), lax.ppermute(b, axis, far))  5.94 us
    ppermute x4, waiting for transfers between devices, exchange(): return (lax.ppermute(a, axis, near), lax.ppermute(b, axis, far))  2.75 us
  transfers between devices with their start and end apart: 4, of which 2 were waited for; matrix products, arithmetic and copies ran while one was open for 0% of the time, Pallas kernels for 7%

profile of v3, /device:TPU:1, one launch (start us, length us, event | category | flops | bytes accessed | tf_op | source)
XLA Modules:
  0.0 48.9 jit_solution(7479977986508134726)
XLA Ops:
  0.0 0.0 copy-start.3
  0.0 0.0 copy-start.2
  0.0 0.0 copy-start
  0.0 0.0 copy-start.1
  0.0 1.7 %shard_map.47 = (f32[116,128]{1,0:T(8,128)}, f32[116,128]{1,0:T(8,128)}) custom-call(f32[2,7,128,128]{3,2,1,0:T(8,128)} %prev.7, f32[2,4,128,128]{3,2,1,0:T(8,128)} %diss.5, s32[4,128,128]{2,1,0:T(8,128)} %mat.7, s32[3,128,128]{2,1,0:T(8,128)} %cool.7), custom_call_target="tpu_custom_call" | custom-call | flops 1048576 | bytes 1048576 | tf_op jit(solution)/shard_map/pallas_call | solution.py:513
  1.8 3.3 %collective-permute-start = (f32[116,128]{1,0:T(8,128)}, f32[116,128]{1,0:T(8,128)S(1)}, u32[]{:S(2)}, u32[]{:S(2)}) collective-permute-start(f32[116,128]{1,0:T(8,128)} %get-tuple-element.23), channel_id=1, source_target_pairs={{0,32},{32,0},{64,96},{96,64},{128,160},{160,128},{192,224},{224,1... | collective-permute-start | bytes 178184 | tf_op jit(solution)/shard_map/ppermute | solution.py:478
  5.0 1.9 %collective-permute-start.1 = (f32[116,128]{1,0:T(8,128)}, f32[116,128]{1,0:T(8,128)S(1)}, u32[]{:S(2)}, u32[]{:S(2)}) collective-permute-start(f32[116,128]{1,0:T(8,128)} %get-tuple-element.24), channel_id=1, source_target_pairs={{32,64},{96,128},{160,192},{64,32},{128,96},{192,160},{33,65},{97,... | collective-permute-start | bytes 178184 | tf_op jit(solution)/shard_map/ppermute | solution.py:478
  7.0 0.0 copy-done.3
  7.0 0.0 copy-done.2
  7.0 0.0 copy-done
  7.0 0.0 copy-done.1
  7.0 1.3 %shard_map.46 = (f32[5,128,128]{2,1,0:T(8,128)S(1)}, f32[7,136,128]{2,1,0:T(8,128)S(1)}, f32[14,152,128]{2,1,0:T(8,128)S(1)}, f32[2,8,128]{2,1,0:T(8,128)S(1)}) custom-call(f32[2,7,128,128]{3,2,1,0:T(8,128)S(1)} %copy-done, f32[2,4,128,128]{3,2,1,0:T(8,128)S(1)} %copy-done.1, s32[4,128,128]{2,1,0:T(8,128)S(1)} %copy-done.2, s32[3,128,128]{2,1,0:T(8,128)S(1)} %copy-done.3), custom_call_target="tpu_custom_call" | custom-call | flops 134217728 | bytes 1048576 | tf_op jit(solution)/shard_map/pallas_call | solution.py:513
  8.3 0.0 collective-permute-done.a_in
  8.3 2.5 %collective-permute-done.1.b_in = f32[116,128]{1,0:T(8,128)S(1)} collective-permute-done((f32[116,128]{1,0:T(8,128)}, f32[116,128]{1,0:T(8,128)S(1)}, u32[]{:S(2)}, u32[]{:S(2)}) %collective-permute-start.1) | collective-permute-done | bytes 59424 | tf_op jit(solution)/shard_map/ppermute | solution.py:478
  10.8 1.2 %shard_map.48 = (f32[136,128]{1,0:T(8,128)S(1)}, f32[136,128]{1,0:T(8,128)S(1)}, f32[29,8,128]{2,1,0:T(8,128)S(1)}, f32[5,8,128]{2,1,0:T(8,128)S(1)}) custom-call(f32[5,128,128]{2,1,0:T(8,128)S(1)} %get-tuple-element.22.c_ref, f32[116,128]{1,0:T(8,128)S(1)} %collective-permute-done.a_in, f32[116,128]{1,0:T(8,128)S(1)} %collective-permute-done.1.b_in), custom_call_target="tpu_custom_call" | custom-call | flops 1048576 | bytes 1048576 | tf_op jit(solution)/shard_map/pallas_call | solution.py:513
  12.0 0.1 collective-permute-start.2
  12.1 0.7 %collective-permute-start.3 = (f32[136,128]{1,0:T(8,128)S(1)}, f32[136,128]{1,0:T(8,128)S(1)}, u32[]{:S(2)}, u32[]{:S(2)}) collective-permute-start(f32[136,128]{1,0:T(8,128)S(1)} %get-tuple-element.33), channel_id=1, source_target_pairs={{1,2},{3,4},{5,6},{7,8},{9,10},{11,12},{13,14},{15,16},{17,18},{19... | collective-permute-start | bytes 208904 | tf_op jit(solution)/shard_map/ppermute | solution.py:478
  12.7 2.2 %shard_map.49 = (f32[14,152,128]{2,1,0:T(8,128)S(1)}, f32[14,152,128]{2,1,0:T(8,128)S(1)}, f32[14,16,128]{2,1,0:T(8,128)S(1)}, f32[12,8,128]{2,1,0:T(8,128)S(1)}) custom-call(f32[2,7,128,128]{3,2,1,0:T(8,128)S(1)} %copy-done, f32[2,4,128,128]{3,2,1,0:T(8,128)S(1)} %copy-done.1, s32[4,128,128]{2,1,0:T(8,128)S(1)} %copy-done.2, s32[3,128,128]{2,1,0:T(8,128)S(1)} %copy-done.3, ...), custom_call_target="tpu_custom_call" | custom-call | flops 134217728 | bytes 1048576 | tf_op jit(solution)/shard_map/pallas_call | solution.py:513
  15.0 0.2 collective-permute-done.2.a_in
  15.2 0.0 collective-permute-done.3.b_in
  15.2 1.7 %shard_map.50 = (f32[6,128,128]{2,1,0:T(8,128)S(1)}, f32[32,8,128]{2,1,0:T(8,128)S(1)}) custom-call(f32[5,128,128]{2,1,0:T(8,128)S(1)} %get-tuple-element.22.c_ref, f32[5,8,128]{2,1,0:T(8,128)S(1)} %get-tuple-element.31.c_halo, f32[136,128]{1,0:T(8,128)S(1)} %collective-permute-done.2.a_in, f32[136,128]{1,0:T(8,128)S(1)} %collective-permute-done.3.b_in, ...), custom_call_target="tpu_custom_call" | custom-call | flops 16777216 | bytes 1048576 | tf_op jit(solution)/shard_map/pallas_call | solution.py:513
  16.9 30.6 %all_to_all.5 = f32[256,1,128]{2,1,0:T(1,128)S(1)} all-to-all(f32[256,1,128]{2,1,0:T(1,128)S(1)} %bitcast.5), channel_id=1, replica_groups=mesh['gx'=8,'gy'=32] {'gx','gy'}, dimensions={0} | all-to-all | bytes 262144 | tf_op jit(solution)/shard_map/all_to_all | solution.py:578
  47.6 1.3 %shard_map.51 = f32[2,7,128,128]{3,2,1,0:T(8,128)} custom-call(f32[2,7,128,128]{3,2,1,0:T(8,128)S(1)} %copy-done, s32[4,128,128]{2,1,0:T(8,128)S(1)} %copy-done.2, s32[3,128,128]{2,1,0:T(8,128)S(1)} %copy-done.3, f32[14,152,128]{2,1,0:T(8,128)S(1)} %get-tuple-element.21.y0, f32[14,16,128]{2,1,0:T(8,128)S(1)} %get-tuple-element.28.y0_fix, ...), custom_call_target="tpu_custom_call" | custom-call | flops 16777216 | bytes 1048576 | tf_op jit(solution)/shard_map/pallas_call | solution.py:513
Async XLA Ops:
  0.0 7.0 %copy-start.3 = (s32[3,128,128]{2,1,0:T(8,128)S(1)}, s32[3,128,128]{2,1,0:T(8,128)}, u32[]{:S(2)}) copy-start(s32[3,128,128]{2,1,0:T(8,128)} %cool.7) | copy-start | bytes 589828
  0.0 7.0 %copy-start.2 = (s32[4,128,128]{2,1,0:T(8,128)S(1)}, s32[4,128,128]{2,1,0:T(8,128)}, u32[]{:S(2)}) copy-start(s32[4,128,128]{2,1,0:T(8,128)} %mat.7) | copy-start | bytes 786436
  0.0 7.0 %copy-start = (f32[2,7,128,128]{3,2,1,0:T(8,128)S(1)}, f32[2,7,128,128]{3,2,1,0:T(8,128)}, u32[]{:S(2)}) copy-start(f32[2,7,128,128]{3,2,1,0:T(8,128)} %prev.7) | copy-start | bytes 2752516
  0.0 7.0 %copy-start.1 = (f32[2,4,128,128]{3,2,1,0:T(8,128)S(1)}, f32[2,4,128,128]{3,2,1,0:T(8,128)}, u32[]{:S(2)}) copy-start(f32[2,4,128,128]{3,2,1,0:T(8,128)} %diss.5) | copy-start | bytes 1572868
  1.8 6.5 %collective-permute-start = (f32[116,128]{1,0:T(8,128)}, f32[116,128]{1,0:T(8,128)S(1)}, u32[]{:S(2)}, u32[]{:S(2)}) collective-permute-start(f32[116,128]{1,0:T(8,128)} %get-tuple-element.23), channel_id=1, source_target_pairs={{0,32},{32,0},{64,96},{96,64},{128,160},{160,128},{192,224},{224,1... | collective-permute-start | bytes 178184 | tf_op jit(solution)/shard_map/ppermute | solution.py:478
  5.0 5.7 %collective-permute-start.1 = (f32[116,128]{1,0:T(8,128)}, f32[116,128]{1,0:T(8,128)S(1)}, u32[]{:S(2)}, u32[]{:S(2)}) collective-permute-start(f32[116,128]{1,0:T(8,128)} %get-tuple-element.24), channel_id=1, source_target_pairs={{32,64},{96,128},{160,192},{64,32},{128,96},{192,160},{33,65},{97,... | collective-permute-start | bytes 178184 | tf_op jit(solution)/shard_map/ppermute | solution.py:478
  12.0 3.2 %collective-permute-start.2 = (f32[136,128]{1,0:T(8,128)S(1)}, f32[136,128]{1,0:T(8,128)S(1)}, u32[]{:S(2)}, u32[]{:S(2)}) collective-permute-start(f32[136,128]{1,0:T(8,128)S(1)} %get-tuple-element.32), channel_id=1, source_target_pairs={{0,1},{1,0},{2,3},{3,2},{4,5},{5,4},{6,7},{7,6},{8,9},{9,8},{10,11... | collective-permute-start | bytes 208904 | tf_op jit(solution)/shard_map/ppermute | solution.py:478
  12.1 3.1 %collective-permute-start.3 = (f32[136,128]{1,0:T(8,128)S(1)}, f32[136,128]{1,0:T(8,128)S(1)}, u32[]{:S(2)}, u32[]{:S(2)}) collective-permute-start(f32[136,128]{1,0:T(8,128)S(1)} %get-tuple-element.33), channel_id=1, source_target_pairs={{1,2},{3,4},{5,6},{7,8},{9,10},{11,12},{13,14},{15,16},{17,18},{19... | collective-permute-start | bytes 208904 | tf_op jit(solution)/shard_map/ppermute | solution.py:478

commit v4 on v3

--- a/solution.py
+++ b/solution.py
@@ -187,15 +187,20 @@
         m_out[scen] = acc[scen]
 
 
-def messages(c_ref, a_in, b_in, a_out, b_out, halo_out, c_halo):
+def messages(rows_of_devices, c_ref, a_in, b_in, a_out, b_out, halo_out, c_halo):
     lower = lax.axis_index("gx") % 2 == 0
     west = lax.axis_index("gy") % 2 == 0
+    at_top, at_bottom = lax.axis_index("gx") == 0, lax.axis_index("gx") == rows_of_devices - 1
     lane = lax.broadcasted_iota(jnp.int32, (8, TILE), 1)
     for field in range(FIELDS):
         rows = slice(HALO * field, HALO * (field + 1))
         a, b = a_in[rows, :], b_in[rows, :]
-        halo_out[field, :HALO, :] = jnp.where(lower, b, a)
-        halo_out[field, HALO:, :] = jnp.where(lower, a, b)
+        above, below = jnp.where(lower, b, a), jnp.where(lower, a, b)
+        if field >= CODE:
+            above = jnp.where(at_top, 0.0, above)
+            below = jnp.where(at_bottom, 0.0, below)
+        halo_out[field, :HALO, :] = above
+        halo_out[field, HALO:, :] = below
     slot = lane % GROUP // HALO
     odd = lane // GROUP % 2 == 1
 
@@ -321,9 +326,10 @@
 ROWS = TOP + TILE + 16
 
 
-def strips(c_ref, c_halo, a_in, b_in, m_in, ys_out, m_out, code_ref, s_ref, x_ref, d_ref, yp_ref, q_ref, y0, y1, y2):
+def strips(columns_of_devices, c_ref, c_halo, a_in, b_in, m_in, ys_out, m_out, code_ref, s_ref, x_ref, d_ref, yp_ref, q_ref, y0, y1, y2):
     west = lax.axis_index("gy") % 2 == 0
     lane = lax.broadcasted_iota(jnp.int32, (8, TILE), 1)
+    outside = [lax.axis_index("gy") == end for end in (columns_of_devices - 1, 0)]
     place = lane % GROUP
     real = lane < GROUP * LAYERS
     tier = lane // GROUP % 2 == 0
@@ -348,6 +354,7 @@
         blocks = [c_halo[i] if rows is None else c_ref[i, rows, :] for i in range(5)]
         for side, (own, beyond, _, base) in enumerate(sides):
             got = jnp.where(west, a, b) if side == 0 else jnp.where(west, b, a)
+            got = jnp.where(outside[side], 0.0, got)
             full = []
             for index, shift in enumerate((base, base - 4, base - 8, base - 12, base - 12 - GROUP)):
                 mask = beyond if index < 3 else beyond & tier
@@ -469,7 +476,7 @@
 
 def swaps(devices):
     near = [(i, i ^ 1) for i in range(devices)]
-    far = [(i, i + 1) for i in range(1, devices - 1, 2)]
+    far = [(i, (i + 1) % devices) for i in range(1, devices, 2)]
     return near, far + [(b, a) for a, b in far]
 
 
@@ -532,10 +539,10 @@
         edges += [buffer(a.dtype, *a.shape[:-2], 8, TILE)] * 2
     a, b = call(
         pack_rows,
-        given,
-        [shape(FIELDS * HALO, TILE)] * 2,
+        [pltpu.with_memory_space_constraint(x, pltpu.HBM) for x in given],
+        [pltpu.VMEM((FIELDS * HALO, TILE), F32)] * 2,
         edges + [pltpu.SemaphoreType.DMA((8,))],
-        62,
+        4,
         1 << 20,
         in_specs=[pl.BlockSpec(memory_space=pltpu.HBM)] * 4,
     )
@@ -550,7 +557,7 @@
         1 << 27,
     )
     a, b, halo, c_halo = call(
-        messages,
+        functools.partial(messages, lax.axis_size("gx")),
         (c_blocks, a, b),
         [shape(TILE + 8, TILE)] * 2 + [shape(FIELDS, 8, TILE), shape(5, 8, TILE)],
         [],
@@ -568,7 +575,7 @@
     )
     devices = lax.axis_size("gx") * lax.axis_size("gy")
     ys, m = call(
-        strips,
+        functools.partial(strips, lax.axis_size("gy")),
         (c_blocks, c_halo, a, b, m),
         [shape(3 * SCEN, TILE, TILE), shape(devices // 8, 8, TILE)],
         [buffer(F32, n, ROWS, TILE) for n in (2, 2, 4, 4, 4, 2, 4, 4, 4)],

time: 49.1 us -> 45.2 us (0.921)
  blocking collectives: 30.6 us -> 23.5 us
  starting transfers between devices: 5.94 us -> 9.87 us
  Pallas kernels: 9.47 us -> 8.91 us
    all_to_all x1, blocking collectives: 30.6 us -> 23.5 us  [per_device(): lax.all_to_all(m.reshape(devices, 1, TILE), ('gx', 'gy'), split_axis=0, c...]
    ppermute x4, starting transfers between devices: 5.94 us -> 9.87 us  [exchange(): return (lax.ppermute(a, axis, near), lax.ppermute(b, axis, far))]
    pallas_call x6, Pallas kernels: 9.47 us -> 8.91 us  [call(): pl.pallas_call(kernel, in_specs=in_specs or vmem(len(inputs)), out_specs=...]
  transfers between devices with their start and end apart: 4 -> 4, of which waited for: 2 -> 1; matrix products, arithmetic and copies ran while one was open for 0% -> 0% of each run, Pallas kernels for 7% -> 8%
where the time goes in v4:
time: 45.2 us; the launch traced here: 45.1 us
  blocking collectives  23.5 us (52%)
  starting transfers between devices  9.87 us (22%)
  Pallas kernels  8.91 us (20%)
  waiting for transfers between devices  2.63 us (6%)
    all_to_all x1, blocking collectives, per_device(): lax.all_to_all(m.reshape(devices, 1, TILE), ('gx', 'gy'), split_axis=0, c...  23.5 us
    ppermute x4, starting transfers between devices, exchange(): return (lax.ppermute(a, axis, near), lax.ppermute(b, axis, far))  9.87 us
    pallas_call x6, Pallas kernels, call(): pl.pallas_call(kernel, in_specs=in_specs or vmem(len(inputs)), out_specs=...  8.91 us
    ppermute x4, waiting for transfers between devices, exchange(): return (lax.ppermute(a, axis, near), lax.ppermute(b, axis, far))  2.63 us
  transfers between devices with their start and end apart: 4, of which 1 were waited for; matrix products, arithmetic and copies ran while one was open for 0% of the time, Pallas kernels for 8%

profile of v4, /device:TPU:1, one launch (start us, length us, event | category | flops | bytes accessed | tf_op | source)
XLA Modules:
  0.0 45.1 jit_solution(2879546768588861397)
XLA Ops:
  0.0 0.0 copy-start.3
  0.0 0.0 copy-start.2
  0.0 0.0 copy-start
  0.0 0.0 copy-start.1
  0.0 1.1 %shard_map.47 = (f32[116,128]{1,0:T(8,128)S(1)}, f32[116,128]{1,0:T(8,128)S(1)}) custom-call(f32[2,7,128,128]{3,2,1,0:T(8,128)} %prev.7, f32[2,4,128,128]{3,2,1,0:T(8,128)} %diss.5, s32[4,128,128]{2,1,0:T(8,128)} %mat.7, s32[3,128,128]{2,1,0:T(8,128)} %cool.7), custom_call_target="tpu_custom_call" | custom-call | flops 1048576 | bytes 1048576 | tf_op jit(solution)/shard_map/pallas_call | solution.py:520
  1.1 3.3 %collective-permute-start = (f32[116,128]{1,0:T(8,128)S(1)}, f32[116,128]{1,0:T(8,128)S(1)}, u32[]{:S(2)}, u32[]{:S(2)}) collective-permute-start(f32[116,128]{1,0:T(8,128)S(1)} %get-tuple-element.23), channel_id=1, source_target_pairs={{0,32},{32,0},{64,96},{96,64},{128,160},{160,128},{192,224},{224,1... | collective-permute-start | bytes 178184 | tf_op jit(solution)/shard_map/ppermute | solution.py:485
  4.4 0.0 collective-permute-start.1
  4.4 0.0 copy-done.3
  4.4 0.0 copy-done.2
  4.4 0.0 copy-done
  4.4 0.0 copy-done.1
  4.4 1.3 %shard_map.46 = (f32[5,128,128]{2,1,0:T(8,128)S(1)}, f32[7,136,128]{2,1,0:T(8,128)S(1)}, f32[14,152,128]{2,1,0:T(8,128)S(1)}, f32[2,8,128]{2,1,0:T(8,128)S(1)}) custom-call(f32[2,7,128,128]{3,2,1,0:T(8,128)S(1)} %copy-done, f32[2,4,128,128]{3,2,1,0:T(8,128)S(1)} %copy-done.1, s32[4,128,128]{2,1,0:T(8,128)S(1)} %copy-done.2, s32[3,128,128]{2,1,0:T(8,128)S(1)} %copy-done.3), custom_call_target="tpu_custom_call" | custom-call | flops 134217728 | bytes 1048576 | tf_op jit(solution)/shard_map/pallas_call | solution.py:520
  5.7 0.0 collective-permute-done.a_in
  5.7 2.6 %collective-permute-done.1.b_in = f32[116,128]{1,0:T(8,128)S(1)} collective-permute-done((f32[116,128]{1,0:T(8,128)S(1)}, f32[116,128]{1,0:T(8,128)S(1)}, u32[]{:S(2)}, u32[]{:S(2)}) %collective-permute-start.1) | collective-permute-done | bytes 59424 | tf_op jit(solution)/shard_map/ppermute | solution.py:485
  8.3 1.2 %shard_map.48 = (f32[136,128]{1,0:T(8,128)S(1)}, f32[136,128]{1,0:T(8,128)S(1)}, f32[29,8,128]{2,1,0:T(8,128)S(1)}, f32[5,8,128]{2,1,0:T(8,128)S(1)}) custom-call(f32[5,128,128]{2,1,0:T(8,128)S(1)} %get-tuple-element.22.c_ref, f32[116,128]{1,0:T(8,128)S(1)} %collective-permute-done.a_in, f32[116,128]{1,0:T(8,128)S(1)} %collective-permute-done.1.b_in), custom_call_target="tpu_custom_call" | custom-call | flops 1048576 | bytes 1048576 | tf_op jit(solution)/shard_map/pallas_call | solution.py:520
  9.5 0.1 collective-permute-start.2
  9.6 6.5 %collective-permute-start.3 = (f32[136,128]{1,0:T(8,128)S(1)}, f32[136,128]{1,0:T(8,128)S(1)}, u32[]{:S(2)}, u32[]{:S(2)}) collective-permute-start(f32[136,128]{1,0:T(8,128)S(1)} %get-tuple-element.33), channel_id=1, source_target_pairs={{1,2},{3,4},{5,6},{7,8},{9,10},{11,12},{13,14},{15,16},{17,18},{19... | collective-permute-start | bytes 208904 | tf_op jit(solution)/shard_map/ppermute | solution.py:485
  16.1 2.3 %shard_map.49 = (f32[14,152,128]{2,1,0:T(8,128)S(1)}, f32[14,152,128]{2,1,0:T(8,128)S(1)}, f32[14,16,128]{2,1,0:T(8,128)S(1)}, f32[12,8,128]{2,1,0:T(8,128)S(1)}) custom-call(f32[2,7,128,128]{3,2,1,0:T(8,128)S(1)} %copy-done, f32[2,4,128,128]{3,2,1,0:T(8,128)S(1)} %copy-done.1, s32[4,128,128]{2,1,0:T(8,128)S(1)} %copy-done.2, s32[3,128,128]{2,1,0:T(8,128)S(1)} %copy-done.3, ...), custom_call_target="tpu_custom_call" | custom-call | flops 134217728 | bytes 1048576 | tf_op jit(solution)/shard_map/pallas_call | solution.py:520
  18.4 0.0 collective-permute-done.2.a_in
  18.4 0.0 collective-permute-done.3.b_in
  18.4 1.7 %shard_map.50 = (f32[6,128,128]{2,1,0:T(8,128)S(1)}, f32[32,8,128]{2,1,0:T(8,128)S(1)}) custom-call(f32[5,128,128]{2,1,0:T(8,128)S(1)} %get-tuple-element.22.c_ref, f32[5,8,128]{2,1,0:T(8,128)S(1)} %get-tuple-element.31.c_halo, f32[136,128]{1,0:T(8,128)S(1)} %collective-permute-done.2.a_in, f32[136,128]{1,0:T(8,128)S(1)} %collective-permute-done.3.b_in, ...), custom_call_target="tpu_custom_call" | custom-call | flops 16777216 | bytes 1048576 | tf_op jit(solution)/shard_map/pallas_call | solution.py:520
  20.2 23.5 %all_to_all.5 = f32[256,1,128]{2,1,0:T(1,128)S(1)} all-to-all(f32[256,1,128]{2,1,0:T(1,128)S(1)} %bitcast.5), channel_id=1, replica_groups=mesh['gx'=8,'gy'=32] {'gx','gy'}, dimensions={0} | all-to-all | bytes 262144 | tf_op jit(solution)/shard_map/all_to_all | solution.py:585
  43.7 1.4 %shard_map.51 = f32[2,7,128,128]{3,2,1,0:T(8,128)} custom-call(f32[2,7,128,128]{3,2,1,0:T(8,128)S(1)} %copy-done, s32[4,128,128]{2,1,0:T(8,128)S(1)} %copy-done.2, s32[3,128,128]{2,1,0:T(8,128)S(1)} %copy-done.3, f32[14,152,128]{2,1,0:T(8,128)S(1)} %get-tuple-element.21.y0, f32[14,16,128]{2,1,0:T(8,128)S(1)} %get-tuple-element.28.y0_fix, ...), custom_call_target="tpu_custom_call" | custom-call | flops 16777216 | bytes 1048576 | tf_op jit(solution)/shard_map/pallas_call | solution.py:520
Async XLA Ops:
  0.0 4.4 %copy-start.3 = (s32[3,128,128]{2,1,0:T(8,128)S(1)}, s32[3,128,128]{2,1,0:T(8,128)}, u32[]{:S(2)}) copy-start(s32[3,128,128]{2,1,0:T(8,128)} %cool.7) | copy-start | bytes 589828
  0.0 4.4 %copy-start.2 = (s32[4,128,128]{2,1,0:T(8,128)S(1)}, s32[4,128,128]{2,1,0:T(8,128)}, u32[]{:S(2)}) copy-start(s32[4,128,128]{2,1,0:T(8,128)} %mat.7) | copy-start | bytes 786436
  0.0 4.4 %copy-start = (f32[2,7,128,128]{3,2,1,0:T(8,128)S(1)}, f32[2,7,128,128]{3,2,1,0:T(8,128)}, u32[]{:S(2)}) copy-start(f32[2,7,128,128]{3,2,1,0:T(8,128)} %prev.7) | copy-start | bytes 2752516
  0.0 4.4 %copy-start.1 = (f32[2,4,128,128]{3,2,1,0:T(8,128)S(1)}, f32[2,4,128,128]{3,2,1,0:T(8,128)}, u32[]{:S(2)}) copy-start(f32[2,4,128,128]{3,2,1,0:T(8,128)} %diss.5) | copy-start | bytes 1572868
  1.1 4.6 %collective-permute-start = (f32[116,128]{1,0:T(8,128)S(1)}, f32[116,128]{1,0:T(8,128)S(1)}, u32[]{:S(2)}, u32[]{:S(2)}) collective-permute-start(f32[116,128]{1,0:T(8,128)S(1)} %get-tuple-element.23), channel_id=1, source_target_pairs={{0,32},{32,0},{64,96},{96,64},{128,160},{160,128},{192,224},{224,1... | collective-permute-start | bytes 178184 | tf_op jit(solution)/shard_map/ppermute | solution.py:485
  4.4 3.9 %collective-permute-start.1 = (f32[116,128]{1,0:T(8,128)S(1)}, f32[116,128]{1,0:T(8,128)S(1)}, u32[]{:S(2)}, u32[]{:S(2)}) collective-permute-start(f32[116,128]{1,0:T(8,128)S(1)} %get-tuple-element.24), channel_id=1, source_target_pairs={{32,64},{96,128},{160,192},{224,0},{64,32},{128,96},{192,160},{0,2... | collective-permute-start | bytes 178184 | tf_op jit(solution)/shard_map/ppermute | solution.py:485
  9.5 8.9 %collective-permute-start.2 = (f32[136,128]{1,0:T(8,128)S(1)}, f32[136,128]{1,0:T(8,128)S(1)}, u32[]{:S(2)}, u32[]{:S(2)}) collective-permute-start(f32[136,128]{1,0:T(8,128)S(1)} %get-tuple-element.32), channel_id=1, source_target_pairs={{0,1},{1,0},{2,3},{3,2},{4,5},{5,4},{6,7},{7,6},{8,9},{9,8},{10,11... | collective-permute-start | bytes 208904 | tf_op jit(solution)/shard_map/ppermute | solution.py:485
  9.6 8.8 %collective-permute-start.3 = (f32[136,128]{1,0:T(8,128)S(1)}, f32[136,128]{1,0:T(8,128)S(1)}, u32[]{:S(2)}, u32[]{:S(2)}) collective-permute-start(f32[136,128]{1,0:T(8,128)S(1)} %get-tuple-element.33), channel_id=1, source_target_pairs={{1,2},{3,4},{5,6},{7,8},{9,10},{11,12},{13,14},{15,16},{17,18},{19... | collective-permute-start | bytes 208904 | tf_op jit(solution)/shard_map/ppermute | solution.py:485

commit v5 on v4

--- a/solution.py
+++ b/solution.py
@@ -105,8 +105,7 @@
         [(layer, layer) for layer in range(LAYERS)],
         [(layer, LAYERS + layer) for layer in range(LAYERS)],
         [(layer, CODE + layer) for layer in range(LAYERS)],
-        [(2 * t, DISS + t) for t in range(TIERS)],
-        [(2 * t, DISS + TIERS + t) for t in range(TIERS)],
+        [(2 * t + scen, DISS + TIERS * scen + t) for t in range(TIERS) for scen in range(SCEN)],
     ):
         out = zero
         for layer, field in fields:
@@ -202,23 +201,22 @@
         halo_out[field, :HALO, :] = above
         halo_out[field, HALO:, :] = below
     slot = lane % GROUP // HALO
-    odd = lane // GROUP % 2 == 1
 
     def send(blocks, rows):
-        def arrange(base):
-            p0, p1, code, d0, d1 = (turn(x, base + HALO * i) for x, i in zip(blocks, (0, 1, 2, 3, 3)))
-            d = jnp.where(odd, turn(d1, GROUP), d0)
-            return jnp.where(slot < 2, jnp.where(slot == 0, p0, p1), jnp.where(slot == 2, code, d))
-
-        low, high = arrange(-8), arrange(-4)
+        p0, p1, code, d = (turn(x, HALO * i - 8) for i, x in enumerate(blocks))
+
+        def by_slot(a, b, c, e):
+            return jnp.where(slot < 2, jnp.where(slot == 0, a, b), jnp.where(slot == 2, c, e))
+
+        low, high = by_slot(p0, p1, code, d), by_slot(p1, code, d, p0)
         a_out[rows, :] = jnp.where(west, high, low)
         b_out[rows, :] = jnp.where(west, low, high)
 
     for k in range(CHUNKS):
         rows = slice(8 * k, 8 * k + 8)
-        send([c_ref[i, rows, :] for i in range(5)], rows)
+        send([c_ref[i, rows, :] for i in range(4)], rows)
     blocks = strips_of(lambda f: halo_out[f], lane)
-    for index in range(5):
+    for index in range(4):
         c_halo[index] = blocks[index]
     send(blocks, slice(TILE, TILE + 8))
 
@@ -334,9 +332,10 @@
     real = lane < GROUP * LAYERS
     tier = lane // GROUP % 2 == 0
     zero = jnp.zeros((8, TILE), F32)
+    slot = place // HALO
     sides = (
-        (place < 8, (place >= 8) & (place < 12) & real, (place >= 4) & (place < 8) & real, 8),
-        (place >= 8, (place >= 4) & (place < 8) & real, (place >= 8) & (place < 12) & real, 4),
+        (place < 8, (place >= 8) & (place < 12), (place >= 4) & (place < 8) & real),
+        (place >= 8, (place >= 4) & (place < 8), (place >= 8) & (place < 12) & real),
     )
 
     def lookup(code, kind):
@@ -351,14 +350,14 @@
     for rows, targets, rotation in chunk_rows:
         message = slice(TILE, TILE + 8) if rows is None else rows
         a, b = a_in[message, :], b_in[message, :]
-        blocks = [c_halo[i] if rows is None else c_ref[i, rows, :] for i in range(5)]
-        for side, (own, beyond, _, base) in enumerate(sides):
-            got = jnp.where(west, a, b) if side == 0 else jnp.where(west, b, a)
-            got = jnp.where(outside[side], 0.0, got)
-            full = []
-            for index, shift in enumerate((base, base - 4, base - 8, base - 12, base - 12 - GROUP)):
-                mask = beyond if index < 3 else beyond & tier
-                full.append(jnp.where(own, blocks[index], jnp.where(mask, turn(got, shift), zero)))
+        blocks = [c_halo[i] if rows is None else c_ref[i, rows, :] for i in range(4)]
+        east = jnp.where(outside[0], 0.0, jnp.where(west, a, b))
+        wst = jnp.where(outside[1], 0.0, jnp.where(west, b, a))
+        got = [turn(jnp.where(slot == i, east, wst), 8 - HALO * i) for i in range(4)]
+        for side, (own, beyond, _) in enumerate(sides):
+            full = [jnp.where(own, x, jnp.where(beyond, y, zero)) for x, y in zip(blocks, got)]
+            full[2] = jnp.where(real, full[2], zero)
+            full[3:] = [jnp.where(tier, full[3], zero), jnp.where(tier, turn(full[3], -GROUP), zero)]
             full = [turn(x, rotation, 0) for x in full]
             s = lookup(full[2], ROOT)
             for at in targets:
@@ -551,7 +550,7 @@
     c_blocks, q, y0, m0 = call(
         begin,
         given,
-        [shape(5, TILE, TILE), shape(LAYERS, TILE + 8, TILE), shape(PAIRS, padded, TILE), shape(SCEN, 8, TILE)],
+        [shape(4, TILE, TILE), shape(LAYERS, TILE + 8, TILE), shape(PAIRS, padded, TILE), shape(SCEN, 8, TILE)],
         [buffer(F32, LAYERS, padded, TILE), buffer(F32, PAIRS, padded, TILE)],
         8,
         1 << 27,
@@ -559,7 +558,7 @@
     a, b, halo, c_halo = call(
         functools.partial(messages, lax.axis_size("gx")),
         (c_blocks, a, b),
-        [shape(TILE + 8, TILE)] * 2 + [shape(FIELDS, 8, TILE), shape(5, 8, TILE)],
+        [shape(TILE + 8, TILE)] * 2 + [shape(FIELDS, 8, TILE), shape(4, 8, TILE)],
         [],
         4,
         1 << 20,

time: 45.2 us -> 44.2 us (0.978)
  Pallas kernels: 8.91 us -> 7.91 us
    pallas_call x6, Pallas kernels: 8.91 us -> 7.91 us  [call(): pl.pallas_call(kernel, in_specs=in_specs or vmem(len(inputs)), out_specs=...]
where the time goes in v5:
time: 44.2 us; the launch traced here: 44 us
  blocking collectives  23.5 us (53%)
  starting transfers between devices  9.86 us (22%)
  Pallas kernels  7.91 us (18%)
  waiting for transfers between devices  2.63 us (6%)
    all_to_all x1, blocking collectives, per_device(): lax.all_to_all(m.reshape(devices, 1, TILE), ('gx', 'gy'), split_axis=0, c...  23.5 us
    ppermute x4, starting transfers between devices, exchange(): return (lax.ppermute(a, axis, near), lax.ppermute(b, axis, far))  9.86 us
    pallas_call x6, Pallas kernels, call(): pl.pallas_call(kernel, in_specs=in_specs or vmem(len(inputs)), out_specs=...  7.91 us
    ppermute x4, waiting for transfers between devices, exchange(): return (lax.ppermute(a, axis, near), lax.ppermute(b, axis, far))  2.63 us
  transfers between devices with their start and end apart: 4, of which 1 were waited for; matrix products, arithmetic and copies ran while one was open for 0% of the time, Pallas kernels for 8%

profile of v5, /device:TPU:1, one launch (start us, length us, event | category | flops | bytes accessed | tf_op | source)
XLA Modules:
  0.0 44.0 jit_solution(12709968756559406709)
XLA Ops:
  0.0 0.0 copy-start.3
  0.0 0.0 copy-start.2
  0.0 0.0 copy-start
  0.0 0.0 copy-start.1
  0.0 1.1 %shard_map.47 = (f32[116,128]{1,0:T(8,128)S(1)}, f32[116,128]{1,0:T(8,128)S(1)}) custom-call(f32[2,7,128,128]{3,2,1,0:T(8,128)} %prev.7, f32[2,4,128,128]{3,2,1,0:T(8,128)} %diss.5, s32[4,128,128]{2,1,0:T(8,128)} %mat.7, s32[3,128,128]{2,1,0:T(8,128)} %cool.7), custom_call_target="tpu_custom_call" | custom-call | flops 1048576 | bytes 1048576 | tf_op jit(solution)/shard_map/pallas_call | solution.py:519
  1.1 3.3 %collective-permute-start = (f32[116,128]{1,0:T(8,128)S(1)}, f32[116,128]{1,0:T(8,128)S(1)}, u32[]{:S(2)}, u32[]{:S(2)}) collective-permute-start(f32[116,128]{1,0:T(8,128)S(1)} %get-tuple-element.23), channel_id=1, source_target_pairs={{0,32},{32,0},{64,96},{96,64},{128,160},{160,128},{192,224},{224,1... | collective-permute-start | bytes 178184 | tf_op jit(solution)/shard_map/ppermute | solution.py:484
  4.4 0.0 collective-permute-start.1
  4.4 0.0 copy-done.3
  4.4 0.0 copy-done.2
  4.4 0.0 copy-done
  4.4 0.0 copy-done.1
  4.4 1.3 %shard_map.46 = (f32[4,128,128]{2,1,0:T(8,128)S(1)}, f32[7,136,128]{2,1,0:T(8,128)S(1)}, f32[14,152,128]{2,1,0:T(8,128)S(1)}, f32[2,8,128]{2,1,0:T(8,128)S(1)}) custom-call(f32[2,7,128,128]{3,2,1,0:T(8,128)S(1)} %copy-done, f32[2,4,128,128]{3,2,1,0:T(8,128)S(1)} %copy-done.1, s32[4,128,128]{2,1,0:T(8,128)S(1)} %copy-done.2, s32[3,128,128]{2,1,0:T(8,128)S(1)} %copy-done.3), custom_call_target="tpu_custom_call" | custom-call | flops 134217728 | bytes 1048576 | tf_op jit(solution)/shard_map/pallas_call | solution.py:519
  5.7 0.0 collective-permute-done.a_in
  5.7 2.6 %collective-permute-done.1.b_in = f32[116,128]{1,0:T(8,128)S(1)} collective-permute-done((f32[116,128]{1,0:T(8,128)S(1)}, f32[116,128]{1,0:T(8,128)S(1)}, u32[]{:S(2)}, u32[]{:S(2)}) %collective-permute-start.1) | collective-permute-done | bytes 59424 | tf_op jit(solution)/shard_map/ppermute | solution.py:484
  8.3 0.2 shard_map.48
  8.5 0.1 collective-permute-start.2
  8.6 6.5 %collective-permute-start.3 = (f32[136,128]{1,0:T(8,128)S(1)}, f32[136,128]{1,0:T(8,128)S(1)}, u32[]{:S(2)}, u32[]{:S(2)}) collective-permute-start(f32[136,128]{1,0:T(8,128)S(1)} %get-tuple-element.33), channel_id=1, source_target_pairs={{1,2},{3,4},{5,6},{7,8},{9,10},{11,12},{13,14},{15,16},{17,18},{19... | collective-permute-start | bytes 208904 | tf_op jit(solution)/shard_map/ppermute | solution.py:484
  15.1 2.3 %shard_map.49 = (f32[14,152,128]{2,1,0:T(8,128)S(1)}, f32[14,152,128]{2,1,0:T(8,128)S(1)}, f32[14,16,128]{2,1,0:T(8,128)S(1)}, f32[12,8,128]{2,1,0:T(8,128)S(1)}) custom-call(f32[2,7,128,128]{3,2,1,0:T(8,128)S(1)} %copy-done, f32[2,4,128,128]{3,2,1,0:T(8,128)S(1)} %copy-done.1, s32[4,128,128]{2,1,0:T(8,128)S(1)} %copy-done.2, s32[3,128,128]{2,1,0:T(8,128)S(1)} %copy-done.3, ...), custom_call_target="tpu_custom_call" | custom-call | flops 134217728 | bytes 1048576 | tf_op jit(solution)/shard_map/pallas_call | solution.py:519
  17.4 0.0 collective-permute-done.2.a_in
  17.4 0.0 collective-permute-done.3.b_in
  17.4 1.7 %shard_map.50 = (f32[6,128,128]{2,1,0:T(8,128)S(1)}, f32[32,8,128]{2,1,0:T(8,128)S(1)}) custom-call(f32[4,128,128]{2,1,0:T(8,128)S(1)} %get-tuple-element.22.c_ref, f32[4,8,128]{2,1,0:T(8,128)S(1)} %get-tuple-element.31.c_halo, f32[136,128]{1,0:T(8,128)S(1)} %collective-permute-done.2.a_in, f32[136,128]{1,0:T(8,128)S(1)} %collective-permute-done.3.b_in, ...), custom_call_target="tpu_custom_call" | custom-call | flops 16777216 | bytes 1048576 | tf_op jit(solution)/shard_map/pallas_call | solution.py:519
  19.1 23.5 %all_to_all.5 = f32[256,1,128]{2,1,0:T(1,128)S(1)} all-to-all(f32[256,1,128]{2,1,0:T(1,128)S(1)} %bitcast.5), channel_id=1, replica_groups=mesh['gx'=8,'gy'=32] {'gx','gy'}, dimensions={0} | all-to-all | bytes 262144 | tf_op jit(solution)/shard_map/all_to_all | solution.py:584
  42.7 1.4 %shard_map.51 = f32[2,7,128,128]{3,2,1,0:T(8,128)} custom-call(f32[2,7,128,128]{3,2,1,0:T(8,128)S(1)} %copy-done, s32[4,128,128]{2,1,0:T(8,128)S(1)} %copy-done.2, s32[3,128,128]{2,1,0:T(8,128)S(1)} %copy-done.3, f32[14,152,128]{2,1,0:T(8,128)S(1)} %get-tuple-element.21.y0, f32[14,16,128]{2,1,0:T(8,128)S(1)} %get-tuple-element.28.y0_fix, ...), custom_call_target="tpu_custom_call" | custom-call | flops 16777216 | bytes 1048576 | tf_op jit(solution)/shard_map/pallas_call | solution.py:519
Async XLA Ops:
  0.0 4.4 %copy-start.3 = (s32[3,128,128]{2,1,0:T(8,128)S(1)}, s32[3,128,128]{2,1,0:T(8,128)}, u32[]{:S(2)}) copy-start(s32[3,128,128]{2,1,0:T(8,128)} %cool.7) | copy-start | bytes 589828
  0.0 4.4 %copy-start.2 = (s32[4,128,128]{2,1,0:T(8,128)S(1)}, s32[4,128,128]{2,1,0:T(8,128)}, u32[]{:S(2)}) copy-start(s32[4,128,128]{2,1,0:T(8,128)} %mat.7) | copy-start | bytes 786436
  0.0 4.4 %copy-start = (f32[2,7,128,128]{3,2,1,0:T(8,128)S(1)}, f32[2,7,128,128]{3,2,1,0:T(8,128)}, u32[]{:S(2)}) copy-start(f32[2,7,128,128]{3,2,1,0:T(8,128)} %prev.7) | copy-start | bytes 2752516
  0.0 4.4 %copy-start.1 = (f32[2,4,128,128]{3,2,1,0:T(8,128)S(1)}, f32[2,4,128,128]{3,2,1,0:T(8,128)}, u32[]{:S(2)}) copy-start(f32[2,4,128,128]{3,2,1,0:T(8,128)} %diss.5) | copy-start | bytes 1572868
  1.1 4.6 %collective-permute-start = (f32[116,128]{1,0:T(8,128)S(1)}, f32[116,128]{1,0:T(8,128)S(1)}, u32[]{:S(2)}, u32[]{:S(2)}) collective-permute-start(f32[116,128]{1,0:T(8,128)S(1)} %get-tuple-element.23), channel_id=1, source_target_pairs={{0,32},{32,0},{64,96},{96,64},{128,160},{160,128},{192,224},{224,1... | collective-permute-start | bytes 178184 | tf_op jit(solution)/shard_map/ppermute | solution.py:484
  4.4 3.9 %collective-permute-start.1 = (f32[116,128]{1,0:T(8,128)S(1)}, f32[116,128]{1,0:T(8,128)S(1)}, u32[]{:S(2)}, u32[]{:S(2)}) collective-permute-start(f32[116,128]{1,0:T(8,128)S(1)} %get-tuple-element.24), channel_id=1, source_target_pairs={{32,64},{96,128},{160,192},{224,0},{64,32},{128,96},{192,160},{0,2... | collective-permute-start | bytes 178184 | tf_op jit(solution)/shard_map/ppermute | solution.py:484
  8.5 8.9 %collective-permute-start.2 = (f32[136,128]{1,0:T(8,128)S(1)}, f32[136,128]{1,0:T(8,128)S(1)}, u32[]{:S(2)}, u32[]{:S(2)}) collective-permute-start(f32[136,128]{1,0:T(8,128)S(1)} %get-tuple-element.32), channel_id=1, source_target_pairs={{0,1},{1,0},{2,3},{3,2},{4,5},{5,4},{6,7},{7,6},{8,9},{9,8},{10,11... | collective-permute-start | bytes 208904 | tf_op jit(solution)/shard_map/ppermute | solution.py:484
  8.6 8.8 %collective-permute-start.3 = (f32[136,128]{1,0:T(8,128)S(1)}, f32[136,128]{1,0:T(8,128)S(1)}, u32[]{:S(2)}, u32[]{:S(2)}) collective-permute-start(f32[136,128]{1,0:T(8,128)S(1)} %get-tuple-element.33), channel_id=1, source_target_pairs={{1,2},{3,4},{5,6},{7,8},{9,10},{11,12},{13,14},{15,16},{17,18},{19... | collective-permute-start | bytes 208904 | tf_op jit(solution)/shard_map/ppermute | solution.py:484

commit v6 on v5

--- a/solution.py
+++ b/solution.py
@@ -79,7 +79,7 @@
     return block.astype(F32) + 1.0
 
 
-def pack_rows(prev, diss, mat, cool, a_out, b_out, pt, pb, dt, db, mt, mb, ct, cb, sems):
+def pack_rows(prev, diss, mat, cool, b_out, a_out, pt, pb, dt, db, mt, mb, ct, cb, sems):
     copies = []
     for index, (source, top, bottom) in enumerate(((prev, pt, pb), (diss, dt, db), (mat, mt, mb), (cool, ct, cb))):
         lead = (slice(None),) * (len(source.shape) - 2)
@@ -186,7 +186,7 @@
         m_out[scen] = acc[scen]
 
 
-def messages(rows_of_devices, c_ref, a_in, b_in, a_out, b_out, halo_out, c_halo):
+def messages(rows_of_devices, c_ref, b_in, a_in, b_out, a_out, halo_out, c_halo):
     lower = lax.axis_index("gx") % 2 == 0
     west = lax.axis_index("gy") % 2 == 0
     at_top, at_bottom = lax.axis_index("gx") == 0, lax.axis_index("gx") == rows_of_devices - 1
@@ -324,7 +324,7 @@
 ROWS = TOP + TILE + 16
 
 
-def strips(columns_of_devices, c_ref, c_halo, a_in, b_in, m_in, ys_out, m_out, code_ref, s_ref, x_ref, d_ref, yp_ref, q_ref, y0, y1, y2):
+def strips(columns_of_devices, c_ref, c_halo, b_in, a_in, m_in, ys_out, m_out, code_ref, s_ref, x_ref, d_ref, yp_ref, q_ref, y0, y1, y2):
     west = lax.axis_index("gy") % 2 == 0
     lane = lax.broadcasted_iota(jnp.int32, (8, TILE), 1)
     outside = [lax.axis_index("gy") == end for end in (columns_of_devices - 1, 0)]
@@ -481,7 +481,8 @@
 
 def exchange(a, b, axis):
     near, far = swaps(lax.axis_size(axis))
-    return lax.ppermute(a, axis, near), lax.ppermute(b, axis, far)
+    b = lax.ppermute(b, axis, far)
+    return lax.ppermute(a, axis, near), b
 
 
 def coefficients(m):
@@ -536,7 +537,7 @@
     edges = []
     for a in given:
         edges += [buffer(a.dtype, *a.shape[:-2], 8, TILE)] * 2
-    a, b = call(
+    b, a = call(
         pack_rows,
         [pltpu.with_memory_space_constraint(x, pltpu.HBM) for x in given],
         [pltpu.VMEM((FIELDS * HALO, TILE), F32)] * 2,
@@ -555,9 +556,9 @@
         8,
         1 << 27,
     )
-    a, b, halo, c_halo = call(
+    b, a, halo, c_halo = call(
         functools.partial(messages, lax.axis_size("gx")),
-        (c_blocks, a, b),
+        (c_blocks, b, a),
         [shape(TILE + 8, TILE)] * 2 + [shape(FIELDS, 8, TILE), shape(4, 8, TILE)],
         [],
         4,
@@ -575,7 +576,7 @@
     devices = lax.axis_size("gx") * lax.axis_size("gy")
     ys, m = call(
         functools.partial(strips, lax.axis_size("gy")),
-        (c_blocks, c_halo, a, b, m),
+        (c_blocks, c_halo, b, a, m),
         [shape(3 * SCEN, TILE, TILE), shape(devices // 8, 8, TILE)],
         [buffer(F32, n, ROWS, TILE) for n in (2, 2, 4, 4, 4, 2, 4, 4, 4)],
         8,

time: 44.2 us -> 43.4 us (0.982)
  starting transfers between devices: 9.86 us -> 11.9 us
  waiting for transfers between devices: 2.63 us -> 0.97 us
  blocking collectives: 23.5 us -> 22.4 us
    ppermute x4, starting transfers between devices: 9.86 us -> 11.9 us  [the longest x2 10.6 us: exchange(): b = lax.ppermute(b, axis, far)]
    ppermute x4, waiting for transfers between devices: 2.63 us -> 0.97 us  [the longest x2 0.96 us: exchange(): return (lax.ppermute(a, axis, near), b)]
    all_to_all x1, blocking collectives: 23.5 us -> 22.4 us  [per_device(): lax.all_to_all(m.reshape(devices, 1, TILE), ('gx', 'gy'), split_axis=0, c...]
where the time goes in v6:
time: 43.4 us; the launch traced here: 43.2 us
  blocking collectives  22.4 us (52%)
  starting transfers between devices  11.9 us (27%)
  Pallas kernels  7.91 us (18%)
  waiting for transfers between devices  0.97 us (2%)
    all_to_all x1, blocking collectives, per_device(): lax.all_to_all(m.reshape(devices, 1, TILE), ('gx', 'gy'), split_axis=0, c...  22.4 us
    ppermute x2, starting transfers between devices, exchange(): b = lax.ppermute(b, axis, far)  10.6 us
    pallas_call x6, Pallas kernels, call(): pl.pallas_call(kernel, in_specs=in_specs or vmem(len(inputs)), out_specs=...  7.91 us
    ppermute x2, starting transfers between devices, exchange(): return (lax.ppermute(a, axis, near), b)  1.27 us
    ppermute x2, waiting for transfers between devices, exchange(): return (lax.ppermute(a, axis, near), b)  0.96 us
  transfers between devices with their start and end apart: 4, of which 1 were waited for; matrix products, arithmetic and copies ran while one was open for 0% of the time, Pallas kernels for 8%

profile of v6, /device:TPU:1, one launch (start us, length us, event | category | flops | bytes accessed | tf_op | source)
XLA Modules:
  0.0 43.2 jit_solution(278823353307895606)
XLA Ops:
  0.0 0.0 copy-start.3
  0.0 0.0 copy-start.2
  0.0 0.0 copy-start
  0.0 0.0 copy-start.1
  0.0 1.1 %shard_map.47 = (f32[116,128]{1,0:T(8,128)S(1)}, f32[116,128]{1,0:T(8,128)S(1)}) custom-call(f32[2,7,128,128]{3,2,1,0:T(8,128)} %prev.7, f32[2,4,128,128]{3,2,1,0:T(8,128)} %diss.5, s32[4,128,128]{2,1,0:T(8,128)} %mat.7, s32[3,128,128]{2,1,0:T(8,128)} %cool.7), custom_call_target="tpu_custom_call" | custom-call | flops 1048576 | bytes 1048576 | tf_op jit(solution)/shard_map/pallas_call | solution.py:520
  1.1 2.8 %collective-permute-start = (f32[116,128]{1,0:T(8,128)S(1)}, f32[116,128]{1,0:T(8,128)S(1)}, u32[]{:S(2)}, u32[]{:S(2)}) collective-permute-start(f32[116,128]{1,0:T(8,128)S(1)} %get-tuple-element.23), channel_id=1, source_target_pairs={{32,64},{96,128},{160,192},{224,0},{64,32},{128,96},{192,160},{0,2... | collective-permute-start | bytes 178184 | tf_op jit(solution)/shard_map/ppermute | solution.py:484
  3.9 1.3 %collective-permute-start.1 = (f32[116,128]{1,0:T(8,128)S(1)}, f32[116,128]{1,0:T(8,128)S(1)}, u32[]{:S(2)}, u32[]{:S(2)}) collective-permute-start(f32[116,128]{1,0:T(8,128)S(1)} %get-tuple-element.24), channel_id=1, source_target_pairs={{0,32},{32,0},{64,96},{96,64},{128,160},{160,128},{192,224},{224,1... | collective-permute-start | bytes 178184 | tf_op jit(solution)/shard_map/ppermute | solution.py:485
  5.2 0.0 copy-done.3
  5.2 0.0 copy-done.2
  5.2 0.0 copy-done
  5.2 0.0 copy-done.1
  5.2 1.3 %shard_map.46 = (f32[4,128,128]{2,1,0:T(8,128)S(1)}, f32[7,136,128]{2,1,0:T(8,128)S(1)}, f32[14,152,128]{2,1,0:T(8,128)S(1)}, f32[2,8,128]{2,1,0:T(8,128)S(1)}) custom-call(f32[2,7,128,128]{3,2,1,0:T(8,128)S(1)} %copy-done, f32[2,4,128,128]{3,2,1,0:T(8,128)S(1)} %copy-done.1, s32[4,128,128]{2,1,0:T(8,128)S(1)} %copy-done.2, s32[3,128,128]{2,1,0:T(8,128)S(1)} %copy-done.3), custom_call_target="tpu_custom_call" | custom-call | flops 134217728 | bytes 1048576 | tf_op jit(solution)/shard_map/pallas_call | solution.py:520
  6.4 0.0 collective-permute-done.b_in
  6.5 0.0 collective-permute-done.1.a_in
  6.5 0.2 shard_map.48
  6.6 7.9 %collective-permute-start.2 = (f32[136,128]{1,0:T(8,128)S(1)}, f32[136,128]{1,0:T(8,128)S(1)}, u32[]{:S(2)}, u32[]{:S(2)}) collective-permute-start(f32[136,128]{1,0:T(8,128)S(1)} %get-tuple-element.32), channel_id=1, source_target_pairs={{1,2},{3,4},{5,6},{7,8},{9,10},{11,12},{13,14},{15,16},{17,18},{19... | collective-permute-start | bytes 208904 | tf_op jit(solution)/shard_map/ppermute | solution.py:484
  14.5 0.0 collective-permute-start.3
  14.5 2.3 %shard_map.49 = (f32[14,152,128]{2,1,0:T(8,128)S(1)}, f32[14,152,128]{2,1,0:T(8,128)S(1)}, f32[14,16,128]{2,1,0:T(8,128)S(1)}, f32[12,8,128]{2,1,0:T(8,128)S(1)}) custom-call(f32[2,7,128,128]{3,2,1,0:T(8,128)S(1)} %copy-done, f32[2,4,128,128]{3,2,1,0:T(8,128)S(1)} %copy-done.1, s32[4,128,128]{2,1,0:T(8,128)S(1)} %copy-done.2, s32[3,128,128]{2,1,0:T(8,128)S(1)} %copy-done.3, ...), custom_call_target="tpu_custom_call" | custom-call | flops 134217728 | bytes 1048576 | tf_op jit(solution)/shard_map/pallas_call | solution.py:520
  16.8 0.0 collective-permute-done.2.b_in
  16.8 1.0 %collective-permute-done.3.a_in = f32[136,128]{1,0:T(8,128)S(1)} collective-permute-done((f32[136,128]{1,0:T(8,128)S(1)}, f32[136,128]{1,0:T(8,128)S(1)}, u32[]{:S(2)}, u32[]{:S(2)}) %collective-permute-start.3) | collective-permute-done | bytes 69664 | tf_op jit(solution)/shard_map/ppermute | solution.py:485
  17.8 1.7 %shard_map.50 = (f32[6,128,128]{2,1,0:T(8,128)S(1)}, f32[32,8,128]{2,1,0:T(8,128)S(1)}) custom-call(f32[4,128,128]{2,1,0:T(8,128)S(1)} %get-tuple-element.22.c_ref, f32[4,8,128]{2,1,0:T(8,128)S(1)} %get-tuple-element.31.c_halo, f32[136,128]{1,0:T(8,128)S(1)} %collective-permute-done.2.b_in, f32[136,128]{1,0:T(8,128)S(1)} %collective-permute-done.3.a_in, ...), custom_call_target="tpu_custom_call" | custom-call | flops 16777216 | bytes 1048576 | tf_op jit(solution)/shard_map/pallas_call | solution.py:520
  19.5 22.4 %all_to_all.5 = f32[256,1,128]{2,1,0:T(1,128)S(1)} all-to-all(f32[256,1,128]{2,1,0:T(1,128)S(1)} %bitcast.5), channel_id=1, replica_groups=mesh['gx'=8,'gy'=32] {'gx','gy'}, dimensions={0} | all-to-all | bytes 262144 | tf_op jit(solution)/shard_map/all_to_all | solution.py:585
  41.9 1.4 %shard_map.51 = f32[2,7,128,128]{3,2,1,0:T(8,128)} custom-call(f32[2,7,128,128]{3,2,1,0:T(8,128)S(1)} %copy-done, s32[4,128,128]{2,1,0:T(8,128)S(1)} %copy-done.2, s32[3,128,128]{2,1,0:T(8,128)S(1)} %copy-done.3, f32[14,152,128]{2,1,0:T(8,128)S(1)} %get-tuple-element.21.y0, f32[14,16,128]{2,1,0:T(8,128)S(1)} %get-tuple-element.28.y0_fix, ...), custom_call_target="tpu_custom_call" | custom-call | flops 16777216 | bytes 1048576 | tf_op jit(solution)/shard_map/pallas_call | solution.py:520
Async XLA Ops:
  0.0 5.2 %copy-start.3 = (s32[3,128,128]{2,1,0:T(8,128)S(1)}, s32[3,128,128]{2,1,0:T(8,128)}, u32[]{:S(2)}) copy-start(s32[3,128,128]{2,1,0:T(8,128)} %cool.7) | copy-start | bytes 589828
  0.0 5.2 %copy-start.2 = (s32[4,128,128]{2,1,0:T(8,128)S(1)}, s32[4,128,128]{2,1,0:T(8,128)}, u32[]{:S(2)}) copy-start(s32[4,128,128]{2,1,0:T(8,128)} %mat.7) | copy-start | bytes 786436
  0.0 5.2 %copy-start = (f32[2,7,128,128]{3,2,1,0:T(8,128)S(1)}, f32[2,7,128,128]{3,2,1,0:T(8,128)}, u32[]{:S(2)}) copy-start(f32[2,7,128,128]{3,2,1,0:T(8,128)} %prev.7) | copy-start | bytes 2752516
  0.0 5.2 %copy-start.1 = (f32[2,4,128,128]{3,2,1,0:T(8,128)S(1)}, f32[2,4,128,128]{3,2,1,0:T(8,128)}, u32[]{:S(2)}) copy-start(f32[2,4,128,128]{3,2,1,0:T(8,128)} %diss.5) | copy-start | bytes 1572868
  1.1 5.3 %collective-permute-start = (f32[116,128]{1,0:T(8,128)S(1)}, f32[116,128]{1,0:T(8,128)S(1)}, u32[]{:S(2)}, u32[]{:S(2)}) collective-permute-start(f32[116,128]{1,0:T(8,128)S(1)} %get-tuple-element.23), channel_id=1, source_target_pairs={{32,64},{96,128},{160,192},{224,0},{64,32},{128,96},{192,160},{0,2... | collective-permute-start | bytes 178184 | tf_op jit(solution)/shard_map/ppermute | solution.py:484
  3.9 2.6 %collective-permute-start.1 = (f32[116,128]{1,0:T(8,128)S(1)}, f32[116,128]{1,0:T(8,128)S(1)}, u32[]{:S(2)}, u32[]{:S(2)}) collective-permute-start(f32[116,128]{1,0:T(8,128)S(1)} %get-tuple-element.24), channel_id=1, source_target_pairs={{0,32},{32,0},{64,96},{96,64},{128,160},{160,128},{192,224},{224,1... | collective-permute-start | bytes 178184 | tf_op jit(solution)/shard_map/ppermute | solution.py:485
  6.6 10.1 %collective-permute-start.2 = (f32[136,128]{1,0:T(8,128)S(1)}, f32[136,128]{1,0:T(8,128)S(1)}, u32[]{:S(2)}, u32[]{:S(2)}) collective-permute-start(f32[136,128]{1,0:T(8,128)S(1)} %get-tuple-element.32), channel_id=1, source_target_pairs={{1,2},{3,4},{5,6},{7,8},{9,10},{11,12},{13,14},{15,16},{17,18},{19... | collective-permute-start | bytes 208904 | tf_op jit(solution)/shard_map/ppermute | solution.py:484
  14.5 3.3 %collective-permute-start.3 = (f32[136,128]{1,0:T(8,128)S(1)}, f32[136,128]{1,0:T(8,128)S(1)}, u32[]{:S(2)}, u32[]{:S(2)}) collective-permute-start(f32[136,128]{1,0:T(8,128)S(1)} %get-tuple-element.33), channel_id=1, source_target_pairs={{0,1},{1,0},{2,3},{3,2},{4,5},{5,4},{6,7},{7,6},{8,9},{9,8},{10,11... | collective-permute-start | bytes 208904 | tf_op jit(solution)/shard_map/ppermute | solution.py:485

commit v7 on v6

--- a/solution.py
+++ b/solution.py
@@ -321,7 +321,7 @@
 
 
 TOP = 16
-ROWS = TOP + TILE + 16
+ROWS = TOP + TILE + 24
 
 
 def strips(columns_of_devices, c_ref, c_halo, b_in, a_in, m_in, ys_out, m_out, code_ref, s_ref, x_ref, d_ref, yp_ref, q_ref, y0, y1, y2):
@@ -436,7 +436,7 @@
         [jnp.broadcast_to(jnp.sum(jnp.where(lane == scen, w, 0.0), axis=1, keepdims=True), (8, TILE)) for w in weights]
         for scen in range(SCEN)
     ]
-    parts = 4
+    parts = 8
     copies = []
 
     def chunk(k, at, first):
@@ -587,7 +587,7 @@
         combine,
         (previous, material, coolant, y0, y0_fix, y1, y2, ys, everything.reshape(devices // 8, 8, TILE)),
         shape(*previous.shape),
-        [buffer(F32, *previous.shape), pltpu.SemaphoreType.DMA((4,))],
+        [buffer(F32, *previous.shape), pltpu.SemaphoreType.DMA((8,))],
         8,
         1 << 24,
         out_specs=pl.BlockSpec(memory_space=pltpu.HBM),

time: 43.4 us -> 43.4 us (level)
  no operation moved by 1% of the time
where the time goes in v7:
time: 43.4 us; the launch traced here: 43.2 us
  blocking collectives  22.4 us (52%)
  starting transfers between devices  11.9 us (27%)
  Pallas kernels  7.91 us (18%)
  waiting for transfers between devices  0.97 us (2%)
    all_to_all x1, blocking collectives, per_device(): lax.all_to_all(m.reshape(devices, 1, TILE), ('gx', 'gy'), split_axis=0, c...  22.4 us
    ppermute x2, starting transfers between devices, exchange(): b = lax.ppermute(b, axis, far)  10.6 us
    pallas_call x6, Pallas kernels, call(): pl.pallas_call(kernel, in_specs=in_specs or vmem(len(inputs)), out_specs=...  7.91 us
    ppermute x2, starting transfers between devices, exchange(): return (lax.ppermute(a, axis, near), b)  1.27 us
    ppermute x2, waiting for transfers between devices, exchange(): return (lax.ppermute(a, axis, near), b)  0.96 us
  transfers between devices with their start and end apart: 4, of which 1 were waited for; matrix products, arithmetic and copies ran while one was open for 0% of the time, Pallas kernels for 8%

profile of v7, /device:TPU:1, one launch (start us, length us, event | category | flops | bytes accessed | tf_op | source)
XLA Modules:
  0.0 43.2 jit_solution(4025034450951187799)
XLA Ops:
  0.0 0.0 copy-start.3
  0.0 0.0 copy-start.2
  0.0 0.0 copy-start
  0.0 0.0 copy-start.1
  0.0 1.1 %shard_map.47 = (f32[116,128]{1,0:T(8,128)S(1)}, f32[116,128]{1,0:T(8,128)S(1)}) custom-call(f32[2,7,128,128]{3,2,1,0:T(8,128)} %prev.7, f32[2,4,128,128]{3,2,1,0:T(8,128)} %diss.5, s32[4,128,128]{2,1,0:T(8,128)} %mat.7, s32[3,128,128]{2,1,0:T(8,128)} %cool.7), custom_call_target="tpu_custom_call" | custom-call | flops 1048576 | bytes 1048576 | tf_op jit(solution)/shard_map/pallas_call | solution.py:520
  1.1 2.8 %collective-permute-start = (f32[116,128]{1,0:T(8,128)S(1)}, f32[116,128]{1,0:T(8,128)S(1)}, u32[]{:S(2)}, u32[]{:S(2)}) collective-permute-start(f32[116,128]{1,0:T(8,128)S(1)} %get-tuple-element.23), channel_id=1, source_target_pairs={{32,64},{96,128},{160,192},{224,0},{64,32},{128,96},{192,160},{0,2... | collective-permute-start | bytes 178184 | tf_op jit(solution)/shard_map/ppermute | solution.py:484
  3.9 1.3 %collective-permute-start.1 = (f32[116,128]{1,0:T(8,128)S(1)}, f32[116,128]{1,0:T(8,128)S(1)}, u32[]{:S(2)}, u32[]{:S(2)}) collective-permute-start(f32[116,128]{1,0:T(8,128)S(1)} %get-tuple-element.24), channel_id=1, source_target_pairs={{0,32},{32,0},{64,96},{96,64},{128,160},{160,128},{192,224},{224,1... | collective-permute-start | bytes 178184 | tf_op jit(solution)/shard_map/ppermute | solution.py:485
  5.2 0.0 copy-done.3
  5.2 0.0 copy-done.2
  5.2 0.0 copy-done
  5.2 0.0 copy-done.1
  5.2 1.3 %shard_map.46 = (f32[4,128,128]{2,1,0:T(8,128)S(1)}, f32[7,136,128]{2,1,0:T(8,128)S(1)}, f32[14,152,128]{2,1,0:T(8,128)S(1)}, f32[2,8,128]{2,1,0:T(8,128)S(1)}) custom-call(f32[2,7,128,128]{3,2,1,0:T(8,128)S(1)} %copy-done, f32[2,4,128,128]{3,2,1,0:T(8,128)S(1)} %copy-done.1, s32[4,128,128]{2,1,0:T(8,128)S(1)} %copy-done.2, s32[3,128,128]{2,1,0:T(8,128)S(1)} %copy-done.3), custom_call_target="tpu_custom_call" | custom-call | flops 134217728 | bytes 1048576 | tf_op jit(solution)/shard_map/pallas_call | solution.py:520
  6.4 0.0 collective-permute-done.b_in
  6.5 0.0 collective-permute-done.1.a_in
  6.5 0.2 shard_map.48
  6.6 7.9 %collective-permute-start.2 = (f32[136,128]{1,0:T(8,128)S(1)}, f32[136,128]{1,0:T(8,128)S(1)}, u32[]{:S(2)}, u32[]{:S(2)}) collective-permute-start(f32[136,128]{1,0:T(8,128)S(1)} %get-tuple-element.32), channel_id=1, source_target_pairs={{1,2},{3,4},{5,6},{7,8},{9,10},{11,12},{13,14},{15,16},{17,18},{19... | collective-permute-start | bytes 208904 | tf_op jit(solution)/shard_map/ppermute | solution.py:484
  14.5 0.0 collective-permute-start.3
  14.5 2.3 %shard_map.49 = (f32[14,152,128]{2,1,0:T(8,128)S(1)}, f32[14,152,128]{2,1,0:T(8,128)S(1)}, f32[14,16,128]{2,1,0:T(8,128)S(1)}, f32[12,8,128]{2,1,0:T(8,128)S(1)}) custom-call(f32[2,7,128,128]{3,2,1,0:T(8,128)S(1)} %copy-done, f32[2,4,128,128]{3,2,1,0:T(8,128)S(1)} %copy-done.1, s32[4,128,128]{2,1,0:T(8,128)S(1)} %copy-done.2, s32[3,128,128]{2,1,0:T(8,128)S(1)} %copy-done.3, ...), custom_call_target="tpu_custom_call" | custom-call | flops 134217728 | bytes 1048576 | tf_op jit(solution)/shard_map/pallas_call | solution.py:520
  16.8 0.0 collective-permute-done.2.b_in
  16.8 1.0 %collective-permute-done.3.a_in = f32[136,128]{1,0:T(8,128)S(1)} collective-permute-done((f32[136,128]{1,0:T(8,128)S(1)}, f32[136,128]{1,0:T(8,128)S(1)}, u32[]{:S(2)}, u32[]{:S(2)}) %collective-permute-start.3) | collective-permute-done | bytes 69664 | tf_op jit(solution)/shard_map/ppermute | solution.py:485
  17.8 1.7 %shard_map.50 = (f32[6,128,128]{2,1,0:T(8,128)S(1)}, f32[32,8,128]{2,1,0:T(8,128)S(1)}) custom-call(f32[4,128,128]{2,1,0:T(8,128)S(1)} %get-tuple-element.22.c_ref, f32[4,8,128]{2,1,0:T(8,128)S(1)} %get-tuple-element.31.c_halo, f32[136,128]{1,0:T(8,128)S(1)} %collective-permute-done.2.b_in, f32[136,128]{1,0:T(8,128)S(1)} %collective-permute-done.3.a_in, ...), custom_call_target="tpu_custom_call" | custom-call | flops 16777216 | bytes 1048576 | tf_op jit(solution)/shard_map/pallas_call | solution.py:520
  19.5 22.4 %all_to_all.5 = f32[256,1,128]{2,1,0:T(1,128)S(1)} all-to-all(f32[256,1,128]{2,1,0:T(1,128)S(1)} %bitcast.5), channel_id=1, replica_groups=mesh['gx'=8,'gy'=32] {'gx','gy'}, dimensions={0} | all-to-all | bytes 262144 | tf_op jit(solution)/shard_map/all_to_all | solution.py:585
  41.9 1.3 %shard_map.51 = f32[2,7,128,128]{3,2,1,0:T(8,128)} custom-call(f32[2,7,128,128]{3,2,1,0:T(8,128)S(1)} %copy-done, s32[4,128,128]{2,1,0:T(8,128)S(1)} %copy-done.2, s32[3,128,128]{2,1,0:T(8,128)S(1)} %copy-done.3, f32[14,152,128]{2,1,0:T(8,128)S(1)} %get-tuple-element.21.y0, f32[14,16,128]{2,1,0:T(8,128)S(1)} %get-tuple-element.28.y0_fix, ...), custom_call_target="tpu_custom_call" | custom-call | flops 16777216 | bytes 1048576 | tf_op jit(solution)/shard_map/pallas_call | solution.py:520
Async XLA Ops:
  0.0 5.2 %copy-start.3 = (s32[3,128,128]{2,1,0:T(8,128)S(1)}, s32[3,128,128]{2,1,0:T(8,128)}, u32[]{:S(2)}) copy-start(s32[3,128,128]{2,1,0:T(8,128)} %cool.7) | copy-start | bytes 589828
  0.0 5.2 %copy-start.2 = (s32[4,128,128]{2,1,0:T(8,128)S(1)}, s32[4,128,128]{2,1,0:T(8,128)}, u32[]{:S(2)}) copy-start(s32[4,128,128]{2,1,0:T(8,128)} %mat.7) | copy-start | bytes 786436
  0.0 5.2 %copy-start = (f32[2,7,128,128]{3,2,1,0:T(8,128)S(1)}, f32[2,7,128,128]{3,2,1,0:T(8,128)}, u32[]{:S(2)}) copy-start(f32[2,7,128,128]{3,2,1,0:T(8,128)} %prev.7) | copy-start | bytes 2752516
  0.0 5.2 %copy-start.1 = (f32[2,4,128,128]{3,2,1,0:T(8,128)S(1)}, f32[2,4,128,128]{3,2,1,0:T(8,128)}, u32[]{:S(2)}) copy-start(f32[2,4,128,128]{3,2,1,0:T(8,128)} %diss.5) | copy-start | bytes 1572868
  1.1 5.3 %collective-permute-start = (f32[116,128]{1,0:T(8,128)S(1)}, f32[116,128]{1,0:T(8,128)S(1)}, u32[]{:S(2)}, u32[]{:S(2)}) collective-permute-start(f32[116,128]{1,0:T(8,128)S(1)} %get-tuple-element.23), channel_id=1, source_target_pairs={{32,64},{96,128},{160,192},{224,0},{64,32},{128,96},{192,160},{0,2... | collective-permute-start | bytes 178184 | tf_op jit(solution)/shard_map/ppermute | solution.py:484
  3.9 2.6 %collective-permute-start.1 = (f32[116,128]{1,0:T(8,128)S(1)}, f32[116,128]{1,0:T(8,128)S(1)}, u32[]{:S(2)}, u32[]{:S(2)}) collective-permute-start(f32[116,128]{1,0:T(8,128)S(1)} %get-tuple-element.24), channel_id=1, source_target_pairs={{0,32},{32,0},{64,96},{96,64},{128,160},{160,128},{192,224},{224,1... | collective-permute-start | bytes 178184 | tf_op jit(solution)/shard_map/ppermute | solution.py:485
  6.6 10.1 %collective-permute-start.2 = (f32[136,128]{1,0:T(8,128)S(1)}, f32[136,128]{1,0:T(8,128)S(1)}, u32[]{:S(2)}, u32[]{:S(2)}) collective-permute-start(f32[136,128]{1,0:T(8,128)S(1)} %get-tuple-element.32), channel_id=1, source_target_pairs={{1,2},{3,4},{5,6},{7,8},{9,10},{11,12},{13,14},{15,16},{17,18},{19... | collective-permute-start | bytes 208904 | tf_op jit(solution)/shard_map/ppermute | solution.py:484
  14.5 3.3 %collective-permute-start.3 = (f32[136,128]{1,0:T(8,128)S(1)}, f32[136,128]{1,0:T(8,128)S(1)}, u32[]{:S(2)}, u32[]{:S(2)}) collective-permute-start(f32[136,128]{1,0:T(8,128)S(1)} %get-tuple-element.33), channel_id=1, source_target_pairs={{0,1},{1,0},{2,3},{3,2},{4,5},{5,4},{6,7},{7,6},{8,9},{9,8},{10,11... | collective-permute-start | bytes 208904 | tf_op jit(solution)/shard_map/ppermute | solution.py:485
